TPU v7x, 16 devices: a whole 2x2x2 slice. The times are simulated.
16 devices in a mesh: depth: 2 (over z), col: 2 (over y), row: 4 (over x, core).
Axes of the slice: x: 2, y: 2, z: 2, core: 2. Of those that a mesh axis runs over, the one named last changes fastest.
Arguments:
- tokens: bfloat16 [32768, 1280], P(('depth', 'row'), 'col')
- w_up: bfloat16 [1280, 5120], P('row', 'col')
- w_down: bfloat16 [5120, 1280], P('row', 'col')
- grad_out: bfloat16 [32768, 1280], P(('depth', 'row'), 'col')
Outputs:
- output 1: bfloat16 [32768, 1280], P(('depth', 'row'), 'col')
- output 2: bfloat16 [32768, 1280], P(('depth', 'row'), 'col')
- output 3: float32 [1280, 5120], P('row', 'col')
- output 4: float32 [5120, 1280], P('row', 'col')
All inputs are finite; a program needn't handle non-finite values.
Results may differ from a plain program's by a relative error of at most 0.001.
Values are sent between devices in bfloat16 or wider.
A program may use at most 1 GiB of HBM per device.

v0:
```python
import jax
import jax.numpy as jnp
from jax import lax
from jax.experimental import pallas as pl
from jax.experimental.pallas import tpu as pltpu
from jax.sharding import PartitionSpec as P


BF16, F32 = jnp.bfloat16, jnp.float32
VMEM_LIMIT = 60 * 1024 * 1024
SQRT_2_OVER_PI = 0.7978845608028654
CUBIC = 0.044715
NCHUNK = 4
NFIRST = 2
NPIECE1 = 4
PER = 2
NSLOT = 3
PIECE = 256
TILE = 16
SUB = 512
MESH = pl.DeviceIdType.MESH
LAST_LAST = (((1,), (1,)), ((), ()))


def dot(a, b):
    return jnp.dot(a, b, preferred_element_type=F32)


def dot_t(a, b):
    return lax.dot_general(a, b, LAST_LAST, preferred_element_type=F32)


def cost(flops, nbytes, trans=0):
    return pl.CostEstimate(flops=flops, bytes_accessed=nbytes, transcendentals=trans)


def params():
    return pltpu.CompilerParams(vmem_limit_bytes=VMEM_LIMIT)


def gather_body(w1_ref, w2_ref, tok_ref, grad_ref, w1, w2, tok_oth, *rest):
    *cut, v1, v2, vt, vg, send, recv, load, store = rest
    col, row, depth = lax.axis_index("col"), lax.axis_index("row"), lax.axis_index("depth")
    x, core = row // 2, row % 2
    to_core = {"row": 2 * x + (1 - core)}
    to_x = {"row": 2 * (1 - x) + core}
    to_col = {"col": 1 - col}
    to_depth = {"depth": 1 - depth}

    barrier = pltpu.get_barrier_semaphore()
    for dev in (to_core, to_x, to_col, to_depth):
        pl.semaphore_signal(barrier, inc=1, device_id=dev, device_id_type=MESH)
    pl.semaphore_wait(barrier, 4)

    def place(which, bx, bcol, at_col, half=None):
        ref = (w1_ref, w2_ref)[which]
        n, m = ref.shape
        side = (bx + at_col) % 2 if which == 0 else (bcol + at_col) % 2
        if which == 0:
            r0, c0 = side * (2 * n) + core * n, bcol * m
        else:
            r0, c0 = (2 * bx + core) * n, side * m
        if half is not None:
            r0, n = r0 + half * (n // 2), n // 2
        return (w1, w2)[which].at[pl.ds(pl.multiple_of(r0, 32), n), pl.ds(pl.multiple_of(c0, 128), m)]

    made = []

    def start(src, dst, dev):
        i = len(made)
        cp = pltpu.make_async_remote_copy(src_ref=src, dst_ref=dst, send_sem=send.at[i], recv_sem=recv.at[i],
                                          device_id=dev, device_id_type=MESH)
        cp.start()
        made.append(cp)
        return cp

    def forward(piece, dev):
        return start(piece, piece, dev)

    def half_of(ref):
        n = ref.shape[0] // 2
        return ref.at[pl.ds(pl.multiple_of(depth * n, 32), n), :]

    late = []

    def to_partner(piece):
        late.append(forward(piece, to_core))

    other = 1 - col
    col1 = start(half_of(w1_ref), place(0, x, col, other, depth), to_col)
    x1 = start(w1_ref, place(0, x, col, col), to_x)
    col2 = start(half_of(w2_ref), place(1, x, col, other, depth), to_col)
    first = tok_oth.shape[0]
    late.append(start(tok_ref.at[pl.ds(0, first), :], tok_oth, to_col))
    late.append(start(w1_ref, place(0, x, col, col), to_core))
    late.append(start(w2_ref, place(1, x, col, col), to_core))
    size = tok_oth.shape[0] // NFIRST
    rest_of = tok_ref.shape[0] - NFIRST * size
    loads = [pltpu.make_async_copy(w1_ref, v1, load.at[0]), pltpu.make_async_copy(w2_ref, v2, load.at[1]),
             pltpu.make_async_copy(tok_ref.at[pl.ds(NFIRST * size, rest_of), :], vt, load.at[2]),
             pltpu.make_async_copy(grad_ref, vg, load.at[3])]
    for cp in loads:
        cp.start()
    for cp in loads:
        cp.wait()
    keep = [pltpu.make_async_copy(v1, place(0, x, col, col), store.at[0]),
            pltpu.make_async_copy(v2, place(1, x, col, col), store.at[1])]
    spans = [(vt, i) for i in range(NCHUNK - NFIRST)] + [(vg, i) for i in range(NCHUNK)]
    for j, (src, i) in enumerate(spans):
        keep.append(pltpu.make_async_copy(src.at[pl.ds(i * size, size), :], cut[j], store.at[2 + j]))
    for cp in keep:
        cp.start()

    def oth(which, bx, half):
        return place(which, bx, other, col, half)

    col1.wait_recv()
    z1 = forward(oth(0, x, depth), to_depth)
    x1h = forward(oth(0, x, depth), to_x)
    to_partner(oth(0, x, depth))
    x2 = start(half_of(w2_ref), place(1, x, col, col, depth), to_x)
    col2.wait_recv()
    z2 = forward(oth(1, x, depth), to_depth)
    x2h = forward(oth(1, x, depth), to_x)
    to_partner(oth(1, x, depth))
    z1.wait_recv()
    to_partner(oth(0, x, 1 - depth))
    x1.wait_recv()
    to_partner(place(0, 1 - x, col, col))
    x1h.wait_recv()
    z1d = forward(oth(0, 1 - x, depth), to_depth)
    to_partner(oth(0, 1 - x, depth))
    z2.wait_recv()
    to_partner(oth(1, x, 1 - depth))
    x2.wait_recv()
    z2o = forward(place(1, 1 - x, col, col, depth), to_depth)
    to_partner(place(1, 1 - x, col, col, depth))
    z1d.wait_recv()
    to_partner(oth(0, 1 - x, 1 - depth))
    x2h.wait_recv()
    z2d = forward(oth(1, 1 - x, depth), to_depth)
    to_partner(oth(1, 1 - x, depth))
    z2o.wait_recv()
    to_partner(place(1, 1 - x, col, col, 1 - depth))
    z2d.wait_recv()
    to_partner(oth(1, 1 - x, 1 - depth))
    for cp in late:
        cp.wait_recv()
    for cp in made:
        cp.wait_send()
    for cp in keep:
        cp.wait()


NCOPY = 25
NCUT = 2 * NCHUNK - NFIRST


def gather_kernel(up, down, tok, grad, rows):
    piece = jax.ShapeDtypeStruct((rows, tok.shape[1]), BF16)
    return pl.pallas_call(
        gather_body,
        in_specs=[pl.BlockSpec(memory_space=pl.ANY)] * 4,
        out_specs=[pl.BlockSpec(memory_space=pl.ANY)] * (3 + NCUT),
        out_shape=[jax.ShapeDtypeStruct((4 * up.shape[0], 2 * up.shape[1]), BF16),
                   jax.ShapeDtypeStruct((4 * down.shape[0], 2 * down.shape[1]), BF16),
                   jax.ShapeDtypeStruct((NFIRST * rows, tok.shape[1]), BF16)] + [piece] * NCUT,
        scratch_shapes=[pltpu.VMEM(up.shape, BF16), pltpu.VMEM(down.shape, BF16),
                        pltpu.VMEM(((NCHUNK - NFIRST) * rows, tok.shape[1]), BF16), pltpu.VMEM(grad.shape, BF16),
                        pltpu.SemaphoreType.DMA((NCOPY,)), pltpu.SemaphoreType.DMA((NCOPY,)),
                        pltpu.SemaphoreType.DMA((4,)), pltpu.SemaphoreType.DMA((2 + NCUT,))],
        compiler_params=pltpu.CompilerParams(collective_id=0, has_side_effects=True, vmem_limit_bytes=VMEM_LIMIT),
        cost_estimate=cost(0, 300_000_000),
        name="gather",
    )(up, down, tok, grad)


ANY = pl.BlockSpec(memory_space=pl.ANY)


def make_up_body(first_row, nlater):
    def up_body(xo_ref, *rest):
        xt_refs, w_ref = rest[:nlater], rest[nlater]
        a_hbm, d_hbm, x_ref, u0_ref, u1_ref, a_ref, d_ref, sem = rest[-8:]
        rows, hh = a_ref.shape[1], xo_ref.shape[1]
        piece = u0_ref.shape[0]
        last = rows // piece - 1
        bn = w_ref.shape[1]
        j, n = pl.program_id(0) * PER + pl.program_id(1), pl.num_programs(0) * PER
        row = pl.multiple_of(pl.program_id(1) * rows, rows)

        def copies(step, part):
            slot = lax.rem(step, NSLOT)
            cols = pl.ds(pl.multiple_of(lax.div(step, PER) * bn, bn), bn)
            base = pl.multiple_of(first_row + lax.rem(step, PER) * rows, rows)
            first, size = ((0, last * piece), (last * piece, piece))[part]
            src, dst = pl.ds(first, size), pl.ds(base + first, size)
            return (pltpu.make_async_copy(a_ref.at[slot, src], a_hbm.at[dst, cols], sem.at[0, part, slot]),
                    pltpu.make_async_copy(d_ref.at[slot, src], d_hbm.at[dst, cols], sem.at[1, part, slot]))

        def start(step, part):
            for cp in copies(step, part):
                cp.start()

        def wait(step, part):
            for cp in copies(step, part):
                cp.wait()

        def finish(u_ref, slot, which):
            for r in range(0, piece, TILE):
                u = u_ref[pl.ds(r, TILE), :]
                sl = pl.ds(which * piece + r, TILE)
                u2 = u * u
                t = jnp.tanh(u * (SQRT_2_OVER_PI + (SQRT_2_OVER_PI * CUBIC) * u2))
                h = 0.5 + 0.5 * t
                a_ref[slot, sl, :] = (u * h).astype(BF16)
                slope = 0.5 * SQRT_2_OVER_PI + (1.5 * SQRT_2_OVER_PI * CUBIC) * u2
                d_ref[slot, sl, :] = h + ((1.0 - t * t) * u) * slope

        @pl.when(j == 0)
        def _():
            x_ref[:, :hh] = xo_ref[...]
            at = 0
            for ref in xt_refs:
                x_ref[at:at + ref.shape[0], hh:] = ref[...]
                at += ref.shape[0]

        @pl.when(j >= NSLOT)
        def _():
            wait(j - NSLOT, 0)

        @pl.when(j >= NSLOT + 1)
        def _():
            wait(j - NSLOT - 1, 1)

        slot, prev = lax.rem(j, NSLOT), lax.rem(j + NSLOT - 1, NSLOT)
        held = (u0_ref, u1_ref)
        for i in range(last + 1):
            held[i % 2][...] = dot(x_ref[pl.ds(row + i * piece, piece), :], w_ref[...])
            if i == 0:
                finish(held[last % 2], prev, last)
            else:
                finish(held[(i - 1) % 2], slot, i - 1)
        start(j, 0)

        @pl.when(j >= 1)
        def _():
            start(j - 1, 1)

        @pl.when(j == n - 1)
        def _():
            wait(j - NSLOT, 1)
            finish(held[last % 2], slot, last)
            start(j, 1)
            for k in range(NSLOT):
                wait(j - k, 0)
                wait(j - k, 1)

    return up_body


def up_kernel(x_own, x_oth, w1, rows, call, bufs, after, bn=512):
    tokens, hh = x_own.shape
    f = w1.shape[1]
    in_specs = [pl.BlockSpec((PER * rows, hh), lambda j, i: (call, 0))]
    in_specs += [pl.BlockSpec(v.shape, lambda j, i: (0, 0)) for v in x_oth]
    in_specs += [pl.BlockSpec((2 * hh, bn), lambda j, i: (0, j))]
    args = [x_own, *x_oth, w1]
    aliases = {}
    if bufs is not None:
        aliases = {len(args): 0, len(args) + 1: 1}
        in_specs += [ANY] * 3
        args += [*bufs, after]
    return pl.pallas_call(
        make_up_body(call * PER * rows, len(x_oth)),
        grid=(f // bn, PER),
        in_specs=in_specs,
        out_specs=[ANY, ANY],
        scratch_shapes=[pltpu.VMEM((PER * rows, 2 * hh), BF16), pltpu.VMEM((PIECE, bn), F32), pltpu.VMEM((PIECE, bn), F32),
                        pltpu.VMEM((NSLOT, rows, bn), BF16), pltpu.VMEM((NSLOT, rows, bn), F32), pltpu.SemaphoreType.DMA((2, 2, NSLOT))],
        out_shape=[jax.ShapeDtypeStruct((tokens, f), BF16), jax.ShapeDtypeStruct((tokens, f), F32)],
        input_output_aliases=aliases,
        compiler_params=params(),
        cost_estimate=cost(2 * PER * rows * 2 * hh * f, PER * rows * f * 6 + 2 * hh * f * 2, PER * rows * f),
        name="up",
    )(*args)


def make_du_body(first_row, nlater):
    def du_body(go_ref, *rest):
        gt_refs, w_ref, d_hbm = rest[:nlater], rest[nlater], rest[nlater + 1]
        u_ref, g_ref, d_ref, a0_ref, a1_ref, sem = rest[-6:]
        rows, hh = u_ref.shape[0], go_ref.shape[1]
        bn = w_ref.shape[0]
        j, n = pl.program_id(0) * PER + pl.program_id(1), pl.num_programs(0) * PER
        row = pl.multiple_of(pl.program_id(1) * rows, rows)

        def copy(step):
            slot = lax.rem(step, NSLOT)
            cols = pl.ds(pl.multiple_of(lax.div(step, PER) * bn, bn), bn)
            base = pl.multiple_of(first_row + lax.rem(step, PER) * rows, rows)
            return pltpu.make_async_copy(d_hbm.at[pl.ds(base, rows), cols], d_ref.at[slot], sem.at[slot])

        @pl.when(j == 0)
        def _():
            for k in range(NSLOT - 1):
                copy(k).start()
            g_ref[:, :hh] = go_ref[...]
            at = 0
            for ref in gt_refs:
                g_ref[at:at + ref.shape[0], hh:] = ref[...]
                at += ref.shape[0]

        @pl.when(j + NSLOT - 1 < n)
        def _():
            copy(j + NSLOT - 1).start()

        copy(j).wait()
        slot = lax.rem(j, NSLOT)
        held = (a0_ref, a1_ref)
        blocks = [(i, k) for k in range(bn // SUB) for i in range(rows // SUB)]

        def finish(ref, i, k):
            for r in range(0, SUB, TILE):
                sl, sk = pl.ds(i * SUB + r, TILE), pl.ds(k * SUB, SUB)
                u_ref[sl, sk] = (ref[pl.ds(r, TILE), :] * d_ref[slot, sl, sk]).astype(BF16)

        for m, (i, k) in enumerate(blocks):
            held[m % 2][...] = dot_t(g_ref[pl.ds(row + i * SUB, SUB), :], w_ref[pl.ds(k * SUB, SUB), :])
            if m:
                finish(held[(m - 1) % 2], *blocks[m - 1])
        finish(held[(len(blocks) - 1) % 2], *blocks[-1])

    return du_body


def du_kernel(g_own, g_oth, w2, d, rows, call, buf, after, bn=1024):
    tokens, hh = g_own.shape
    f = w2.shape[0]
    in_specs = [pl.BlockSpec((PER * rows, hh), lambda j, i: (call, 0))]
    in_specs += [pl.BlockSpec(v.shape, lambda j, i: (0, 0)) for v in g_oth]
    in_specs += [pl.BlockSpec((bn, 2 * hh), lambda j, i: (j, 0)), ANY, ANY]
    args = [g_own, *g_oth, w2, d, after if buf is None else buf]
    return pl.pallas_call(
        make_du_body(call * PER * rows, len(g_oth)),
        grid=(f // bn, PER),
        in_specs=in_specs,
        out_specs=pl.BlockSpec((rows, bn), lambda j, i: (call * PER + i, j)),
        scratch_shapes=[pltpu.VMEM((PER * rows, 2 * hh), BF16), pltpu.VMEM((NSLOT, rows, bn), F32),
                        pltpu.VMEM((SUB, SUB), F32), pltpu.VMEM((SUB, SUB), F32), pltpu.SemaphoreType.DMA((NSLOT,))],
        out_shape=jax.ShapeDtypeStruct((tokens, f), BF16),
        input_output_aliases={} if buf is None else {len(args) - 1: 0},
        compiler_params=params(),
        cost_estimate=cost(2 * PER * rows * 2 * hh * f, PER * rows * f * 6 + 2 * hh * f * 2),
        name="du",
    )(*args)


def y_body(a_ref, w_ref, *rest):
    rest[-1][...] = dot(a_ref[...], w_ref[...]).astype(BF16)


def dx_body(u_ref, w_ref, *rest):
    rest[-1][...] = dot_t(w_ref[...], u_ref[...]).astype(BF16).T


def out_kernel(body, name, a, w, w_shape, hh, first, count, buf, after, bm=512):
    tokens, f = a.shape
    if name == "y":
        bm, first, count = bm // 2, 2 * first, 2 * count
    extra = [v for v in (buf, after) if v is not None]
    return pl.pallas_call(
        body,
        grid=(count,),
        in_specs=[pl.BlockSpec((bm, f), lambda i: (first + i, 0)), pl.BlockSpec(w_shape, lambda i: (0, 0))] + [ANY] * len(extra),
        out_specs=pl.BlockSpec((bm, hh), lambda i: (first + i, 0)),
        out_shape=jax.ShapeDtypeStruct((tokens, hh), BF16),
        input_output_aliases={} if buf is None else {2: 0},
        compiler_params=params(),
        cost_estimate=cost(2 * count * bm * f * hh, count * bm * f * 2 + f * hh * 2),
    )(a, w, *extra)


TR = 512


def transpose_into(t_ref, x_ref):
    for i in range(x_ref.shape[0] // TR):
        sl = pl.ds(i * TR, TR)
        t_ref[:, sl] = x_ref[sl, :].T


def dw2_body(s_ref, g_ref, a_ref, dep_ref, mine_ref, theirs_ref, t_ref, o_ref, sem):
    j, n = pl.program_id(0), pl.num_programs(0)
    m = o_ref.shape[2]

    @pl.when(j == 0)
    def _():
        transpose_into(t_ref, g_ref)

    def copy(step, u, to_ref):
        slot = lax.rem(step, 2)
        cols = lax.rem(2 * step + u, n) * m
        return pltpu.make_async_copy(o_ref.at[2 * slot + u], to_ref.at[:, pl.ds(pl.multiple_of(cols, m), m)], sem.at[slot, u])

    @pl.when(j >= 2)
    def _():
        for u in range(2):
            copy(j - 2, u, mine_ref).wait()

    slot = lax.rem(j, 2)
    r = dot(t_ref[...], a_ref[...])
    o_ref[2 * slot] = r[:, :m]
    o_ref[2 * slot + 1] = r[:, m:]
    for u in range(2):
        owner = lax.div(2 * j + u, n)

        @pl.when(owner == s_ref[1])
        def _():
            copy(j, u, mine_ref).start()

        @pl.when(owner != s_ref[1])
        def _():
            copy(j, u, theirs_ref).start()

    @pl.when(j == n - 1)
    def _():
        for k in range(2):
            for u in range(2):
                copy(j - k, u, mine_ref).wait()


def dw2_kernel(idx, g, a, width, after, bn=512):
    tokens, n = g.shape
    steps = width // bn
    shape = jax.ShapeDtypeStruct((n, width // 2), F32)
    return pl.pallas_call(
        dw2_body,
        grid_spec=pltpu.PrefetchScalarGridSpec(
            num_scalar_prefetch=1,
            grid=(steps,),
            in_specs=[
                pl.BlockSpec((tokens, n), lambda j, s: (0, 0)),
                pl.BlockSpec((tokens, bn), lambda j, s: (0, s[0] * steps + j)),
                ANY,
            ],
            out_specs=[ANY, ANY],
            scratch_shapes=[pltpu.VMEM((n, tokens), BF16), pltpu.VMEM((4, n, bn // 2), F32), pltpu.SemaphoreType.DMA((2, 2))]),
        out_shape=[shape, shape],
        compiler_params=params(),
        cost_estimate=cost(2 * tokens * n * width, tokens * (n + width) * 2 + n * width * 4),
        name="dw2",
    )(idx, g, a, after)


def dw1_body(s_ref, own_ref, *rest):
    *oth_refs, u_ref, dep_ref, mine_ref, theirs_ref, x_ref, t_ref, sem = rest

    @pl.when(pl.program_id(0) == 0)
    def _():
        @pl.when(s_ref[0] == 0)
        def _():
            cp = pltpu.make_async_copy(own_ref, x_ref, sem.at[0])
            cp.start()
            cp.wait()

        @pl.when(s_ref[0] != 0)
        def _():
            cps, at = [], 0
            for i, ref in enumerate(oth_refs):
                cps.append(pltpu.make_async_copy(ref, x_ref.at[pl.ds(at, ref.shape[0]), :], sem.at[i]))
                at += ref.shape[0]
            for cp in cps:
                cp.start()
            for cp in cps:
                cp.wait()

        transpose_into(t_ref, x_ref)

    r = dot(t_ref[...], u_ref[...])
    half = r.shape[0] // 2

    @pl.when(s_ref[2] == 0)
    def _():
        mine_ref[...] = r[:half]
        theirs_ref[...] = r[half:]

    @pl.when(s_ref[2] != 0)
    def _():
        mine_ref[...] = r[half:]
        theirs_ref[...] = r[:half]


def dw1_kernel(s, x_own, x_oth, du, width, after, bn=512):
    tokens, hh = x_own.shape
    steps = width // bn
    out_spec = pl.BlockSpec((hh // 2, bn), lambda j, s: (0, j))
    shape = jax.ShapeDtypeStruct((hh // 2, width), F32)
    return pl.pallas_call(
        dw1_body,
        grid_spec=pltpu.PrefetchScalarGridSpec(
            num_scalar_prefetch=1,
            grid=(steps,),
            in_specs=[ANY] * (1 + len(x_oth)) + [pl.BlockSpec((tokens, bn), lambda j, s: (0, s[1] * steps + j)), ANY],
            out_specs=[out_spec, out_spec],
            scratch_shapes=[pltpu.VMEM((tokens, hh), BF16), pltpu.VMEM((hh, tokens), BF16), pltpu.SemaphoreType.DMA((len(x_oth),))]),
        out_shape=[shape, shape],
        compiler_params=params(),
        cost_estimate=cost(2 * tokens * hh * width, tokens * (hh + width) * 2 + hh * width * 4),
        name="dw1",
    )(s, x_own, *x_oth, du, after)


def sum_body(here_ref, got_ref, came_ref, o_ref):
    o_ref[...] = (here_ref[...] + got_ref[...]) + came_ref[...]


def sum_kernel(here, got, came, at, steps):
    n, m = came.shape
    bm = n // steps
    plain = pl.BlockSpec((bm, m), lambda i: (i, 0))
    return pl.pallas_call(
        sum_body,
        grid=(steps,),
        in_specs=[pl.BlockSpec((bm, m), at), pl.BlockSpec((bm, m), at), plain],
        out_specs=plain,
        out_shape=jax.ShapeDtypeStruct((n, m), F32),
        compiler_params=params(),
        cost_estimate=cost(2 * n * m, 16 * n * m),
        name="layer_sum",
    )(here, got, came)


def fin2_body(*refs):
    *ins, o_ref = refs
    at = 0
    for a_ref, b_ref in zip(ins[::2], ins[1::2]):
        n = a_ref.shape[0]
        o_ref[:, at:at + n] = (a_ref[...] + b_ref[...]).T
        at += n


def fin2_kernel(pairs, bn=256):
    width = pairs[0][0].shape[1]
    flat = [v for pair in pairs for v in pair]
    n = sum(v.shape[0] for v in flat) // 2
    return pl.pallas_call(
        fin2_body,
        grid=(width // bn,),
        in_specs=[pl.BlockSpec((v.shape[0], bn), lambda j: (0, j)) for v in flat],
        out_specs=pl.BlockSpec((bn, n), lambda j: (j, 0)),
        out_shape=jax.ShapeDtypeStruct((width, n), F32),
        compiler_params=params(),
        cost_estimate=cost(n * width, 12 * n * width),
        name="fin2",
    )(*flat)


def solution(mesh):
    nx = mesh.shape["row"] // 2
    act_spec = P(("depth", "row"), "col")
    weight_spec = P("row", "col")
    pair = [(0, 1), (1, 0)]
    core_pair = [(r, r ^ 1) for r in range(2 * nx)]
    x_pair = [(r, r ^ 2) for r in range(2 * nx)]

    def over_core(v):
        return lax.ppermute(v, "row", core_pair)

    def over_x(v):
        return lax.ppermute(v, "row", x_pair)

    def over_col(v):
        return lax.ppermute(v, "col", pair)

    def over_depth(v):
        return lax.ppermute(v, "depth", pair)

    def body(tok, up, down, grad):
        col = lax.axis_index("col")
        row = lax.axis_index("row")
        x, core = row // 2, row % 2
        tokens, hh = tok.shape
        rows = tokens // NCHUNK
        fh = up.shape[1]

        w1, w2, tok_first, *cut = gather_kernel(up, down, tok, grad, rows)
        nlater = NCHUNK - NFIRST
        tok_later = [over_col(cut[i]) for i in range(nlater)]
        grad_oth = [over_col(cut[nlater + i]) for i in range(NCHUNK)]

        outs = {"y": None, "dx": None}
        parts = {"y": ((0, 4), (4, 4)), "dx": ((0, 1), (1, 1), (2, 2), (4, 4))}

        def out_part(key, part, after=None):
            args = (y_body, "y", a, w2, (w2.shape[0], hh)) if key == "y" else (dx_body, "dx", du, w1, (hh, w1.shape[1]))
            outs[key] = out_kernel(*args, hh, *parts[key][part], outs[key], after)
            return outs[key]

        a, d = up_kernel(tok, (tok_first,), w1, rows, 0, None, None)
        dep = out_part("y", 0, w1)
        a, d = up_kernel(tok, tok_later, w1, rows, 1, (a, d), dep)

        away = dw2_kernel(jnp.stack([1 - x, core]), grad, a, fh, d)
        here = dw2_kernel(jnp.stack([x, core]), grad, a, fh, away[0])
        got_away = over_core(away[1])
        got_here = over_core(here[1])
        pieces, at = [], 0
        for n in (384, hh - 384):
            came = over_x(away[0][at:at + n] + got_away[at:at + n])
            layer = sum_kernel(here[0], got_here, came, lambda i, at=at: (at // 128 + i, 0), n // 128)
            pieces.append((layer, over_depth(layer)))
            at += n
        dw_down = fin2_kernel(pieces)

        du = None
        for i in range(NCHUNK // PER):
            du = du_kernel(grad, grad_oth[i * PER:(i + 1) * PER], w2, d, rows, i, du, here[0])

        away = dw1_kernel(jnp.stack([(1 - x + col) % 2, col, core]), tok, (tok_first, *tok_later), du, fh, du)
        dep = out_part("dx", 0, away[0])
        here = dw1_kernel(jnp.stack([(x + col) % 2, col, core]), tok, (tok_first, *tok_later), du, fh, dep)
        got_away = over_core(away[1])
        got_here = over_core(here[1])
        cols = []
        w = fh // NPIECE1
        for p in range(NPIECE1):
            sl = slice(p * w, (p + 1) * w)
            out = away[0][:, sl] + got_away[:, sl]
            came = over_x(out)
            layer = sum_kernel(here[0], got_here, came, lambda i, p=p: (i, p), 2)
            cols.append(layer + over_depth(layer))
        dw_up = jnp.concatenate(cols, axis=1)

        out_part("dx", 1, here[0])
        out_part("y", 1, outs["dx"])
        out_part("dx", 2, outs["y"])
        out_part("dx", 3)
        return outs["y"], outs["dx"], dw_up, dw_down

    return jax.shard_map(body, mesh=mesh, in_specs=(act_spec, weight_spec, weight_spec, act_spec),
                         out_specs=(act_spec, act_spec, weight_spec, weight_spec), check_vma=False)
```

profile of v0, /device:TPU:0, one launch (start us, length us, event | category | flops | bytes accessed | tf_op | source)
XLA Modules:
  0.0 648.5 jit_solution(11250884158795647773)
XLA Ops:
  0.6 115.4 %gather.1 = (bf16[1280,5120]{1,0:T(8,128)(2,1)}, bf16[5120,1280]{1,0:T(8,128)(2,1)}, bf16[2048,640]{1,0:T(8,128)(2,1)}, bf16[1024,640]{1,0:T(8,128)(2,1)}, bf16[...) custom-call(bf16[320,2560]{1,0:T(8,128)(2,1)} %w1_ref.1, ...), custom_call_target="tpu_custom_call" | custom-call | bytes 300000000 | tf_op jit(solution)/shard_map/gather/pallas_call | solution.py:161
  116.1 1.4 collective-permute-start
  117.5 0.7 collective-permute-start.1
  118.1 1.4 collective-permute-start.2
  119.5 0.7 collective-permute-start.3
  120.2 1.4 collective-permute-start.4
  121.5 48.4 %up.2 = (bf16[4096,5120]{1,0:T(8,128)(2,1)}, f32[4096,5120]{1,0:T(8,128)}) custom-call(bf16[4096,640]{1,0:T(8,128)(2,1)} %own_ref.3, bf16[2048,640]{1,0:T(8,128)(2,1)} %get-tuple-element.28.rest_0_, bf16[1280,5120]{1,0:T(8,128)(2,1)} %get-tuple-element.27.rest_1_.rest_0_.rest_2_.w_ref), custom_call_target="tpu_custom_call" | custom-call | flops 26843545600 | bytes 76021760 | tf_op jit(solution)/shard_map/up/pallas_call | solution.py:274
  170.0 0.7 pad_add_fusion
  170.6 0.6 add_add_fusion
  171.2 22.1 %shard_map.75.rest_5_.rest_0_ = bf16[4096,640]{1,0:T(8,128)(2,1)} custom-call(bf16[4096,5120]{1,0:T(8,128)(2,1)} %get-tuple-element.29.a_ref.rest_3_, bf16[5120,1280]{1,0:T(8,128)(2,1)} %get-tuple-element.31.w_ref.rest_2_, bf16[1280,5120]{1,0:T(8,128)(2,1)} %get-tuple-element.27.rest_1_.rest_0_.rest_2_.w_ref), custom_call_target="tpu_custom_call" | custom-call | flops 13421772800 | bytes 27525120 | tf_op jit(solution)/shard_map/pallas_call | solution.py:372
  193.3 0.7 collective-permute-start.5
  194.0 0.4 copy-done.2
  194.4 0.7 copy-done.3
  195.2 48.4 %up.3 = (bf16[4096,5120]{1,0:T(8,128)(2,1)}, f32[4096,5120]{1,0:T(8,128)}) custom-call(bf16[4096,640]{1,0:T(8,128)(2,1)} %own_ref.3, bf16[1024,640]{1,0:T(8,128)(2,1)} %copy-done.2, bf16[1024,640]{1,0:T(8,128)(2,1)} %copy-done.3, bf16[1280,5120]{1,0:T(8,128)(2,1)} %get-tuple-element.27.rest_1_.rest_0_.rest_2_.w_ref, ...), custom_call_target="tpu_custom_call", output_to_operand_aliasing={{0}: (4, {}), {1}: (5, {})} | custom-call | flops 26843545600 | bytes 76021760 | tf_op jit(solution)/shard_map/up/pallas_call | solution.py:274
  243.6 21.5 %dw2.2 = (f32[640,1280]{1,0:T(8,128)}, f32[640,1280]{1,0:T(8,128)}) custom-call(s32[2]{0:T(128)} %get-tuple-element.51.s_ref, bf16[4096,640]{1,0:T(8,128)(2,1)} %go_ref.3, bf16[4096,5120]{1,0:T(8,128)(2,1)} %get-tuple-element.32.a_ref, f32[4096,5120]{1,0:T(8,128)} %get-tuple-element.35.dep_ref.rest_3_), custom_call_target="tpu_custom_call" | custom-call | flops 13421772800 | bytes 32768000 | tf_op jit(solution)/shard_map/dw2/pallas_call | solution.py:437
  265.1 0.0 collective-permute-start.17
  265.1 22.0 %dw2.3 = (f32[640,1280]{1,0:T(8,128)}, f32[640,1280]{1,0:T(8,128)}) custom-call(s32[2]{0:T(128)} %get-tuple-element.50.s_ref, bf16[4096,640]{1,0:T(8,128)(2,1)} %go_ref.3, bf16[4096,5120]{1,0:T(8,128)(2,1)} %get-tuple-element.32.a_ref, f32[640,1280]{1,0:T(8,128)} %get-tuple-element.38.dep_ref), custom_call_target="tpu_custom_call" | custom-call | flops 13421772800 | bytes 32768000 | tf_op jit(solution)/shard_map/dw2/pallas_call | solution.py:437
  287.1 0.8 collective-permute-done.5.rest_1_
  288.0 36.4 %du.2.rest_4_ = bf16[4096,5120]{1,0:T(8,128)(2,1)} custom-call(bf16[4096,640]{1,0:T(8,128)(2,1)} %go_ref.3, bf16[1024,640]{1,0:T(8,128)(2,1)} %collective-permute-done.4.rest_0_, bf16[1024,640]{1,0:T(8,128)(2,1)} %collective-permute-done.5.rest_1_, bf16[5120,1280]{1,0:T(8,128)(2,1)} %get-tuple-element.31.w_ref.rest_2_, ...), custom_call_target="tpu_custom_call" | custom-call | flops 26843545600 | bytes 76021760 | tf_op jit(solution)/shard_map/du/pallas_call | solution.py:344
  324.4 36.4 %du.3.rest_3_.rest_4_.u_ref = bf16[4096,5120]{1,0:T(8,128)(2,1)} custom-call(bf16[4096,640]{1,0:T(8,128)(2,1)} %go_ref.3, bf16[1024,640]{1,0:T(8,128)(2,1)} %collective-permute-done.2.rest_0_, bf16[1024,640]{1,0:T(8,128)(2,1)} %collective-permute-done.3.rest_1_, bf16[5120,1280]{1,0:T(8,128)(2,1)} %get-tuple-element.31.w_ref.rest_2_, ...), custom_call_target="tpu_custom_call", output_to_operand_aliasing={{}: (5, {})} | custom-call | flops 26843545600 | bytes 76021760 | tf_op jit(solution)/shard_map/du/pallas_call | solution.py:344
  360.8 23.4 %dw1.2 = (f32[320,2560]{1,0:T(8,128)}, f32[320,2560]{1,0:T(8,128)}) custom-call(s32[3]{0:T(128)} %get-tuple-element.52.s_ref, bf16[4096,640]{1,0:T(8,128)(2,1)} %own_ref.3, bf16[2048,640]{1,0:T(8,128)(2,1)} %get-tuple-element.28.rest_0_, bf16[1024,640]{1,0:T(8,128)(2,1)} %copy-done.2, bf16[1024,640]{1,0:T(8,128)(2,1)} %copy-done.3, ...), custom_call_target="tpu_custom_call" | custom-call | flops 13421772800 | bytes 32768000 | tf_op jit(solution)/shard_map/dw1/pallas_call | solution.py:499
  384.3 8.9 %shard_map.76.rest_4_.rest_0_ = bf16[4096,640]{1,0:T(8,128)(2,1)} custom-call(bf16[4096,5120]{1,0:T(8,128)(2,1)} %du.3.rest_3_.rest_4_.u_ref, bf16[1280,5120]{1,0:T(8,128)(2,1)} %get-tuple-element.27.rest_1_.rest_0_.rest_2_.w_ref, f32[320,2560]{1,0:T(8,128)} %get-tuple-element.40.rest_0_), custom_call_target="tpu_custom_call" | custom-call | flops 3355443200 | bytes 11796480 | tf_op jit(solution)/shard_map/pallas_call | solution.py:372
  393.2 23.2 %dw1.3 = (f32[320,2560]{1,0:T(8,128)}, f32[320,2560]{1,0:T(8,128)}) custom-call(s32[3]{0:T(128)} %get-tuple-element.53.s_ref, bf16[4096,640]{1,0:T(8,128)(2,1)} %own_ref.3, bf16[2048,640]{1,0:T(8,128)(2,1)} %get-tuple-element.28.rest_0_, bf16[1024,640]{1,0:T(8,128)(2,1)} %copy-done.2, bf16[1024,640]{1,0:T(8,128)(2,1)} %copy-done.3, ...), custom_call_target="tpu_custom_call" | custom-call | flops 13421772800 | bytes 32768000 | tf_op jit(solution)/shard_map/dw1/pallas_call | solution.py:499
  416.5 0.7 collective-permute-start.6
  417.1 0.0 collective-permute-start.16
  417.2 3.9 slice_add_fusion
  421.1 1.3 collective-permute-start.18
  422.4 3.5 slice_add_fusion.5
  425.9 0.7 collective-permute-start.14
  426.6 8.9 %shard_map.77.rest_1_.rest_0_ = bf16[4096,640]{1,0:T(8,128)(2,1)} custom-call(bf16[4096,5120]{1,0:T(8,128)(2,1)} %du.3.rest_3_.rest_4_.u_ref, bf16[1280,5120]{1,0:T(8,128)(2,1)} %get-tuple-element.27.rest_1_.rest_0_.rest_2_.w_ref, bf16[4096,640]{1,0:T(8,128)(2,1)} %shard_map.76.rest_4_.rest_0_, ...), custom_call_target="tpu_custom_call", output_to_operand_aliasing={{}: (2, {})} | custom-call | flops 3355443200 | bytes 11796480 | tf_op jit(solution)/shard_map/pallas_call | solution.py:372
  435.5 1.3 collective-permute-start.12
  436.8 2.9 slice_add_fusion.1
  439.8 0.7 collective-permute-start.10
  440.5 44.2 %collective-permute-done.14.came_ref = f32[320,640]{1,0:T(8,128)} collective-permute-done((f32[320,640]{1,0:T(8,128)}, f32[320,640]{1,0:T(8,128)}, u32[]{:S(2)}, u32[]{:S(2)}) %collective-permute-start.14) | collective-permute-done | bytes 819232 | tf_op jit(solution)/shard_map/ppermute | solution.py:571
  484.6 1.3 collective-permute-start.8
  486.0 2.5 layer_sum.9
  488.4 0.7 collective-permute-start.20
  489.1 0.5 collective-permute-start.15
  489.6 22.2 %shard_map.78.rest_1_ = bf16[4096,640]{1,0:T(8,128)(2,1)} custom-call(bf16[4096,5120]{1,0:T(8,128)(2,1)} %get-tuple-element.32.a_ref, bf16[5120,1280]{1,0:T(8,128)(2,1)} %get-tuple-element.31.w_ref.rest_2_, bf16[4096,640]{1,0:T(8,128)(2,1)} %shard_map.75.rest_5_.rest_0_, bf16[4096,640]{1,0:T(8,128)(2,1)} %shard_map.77.rest_1_.rest_0_), custom_call_target="tpu_custom_call", output_to_operand_aliasing={{}: (2, {})} | custom-call | flops 13421772800 | bytes 27525120 | tf_op jit(solution)/shard_map/pallas_call | solution.py:372
  511.8 4.6 layer_sum.10.refs_0_
  516.5 1.5 collective-permute-start.19
  518.0 12.8 %shard_map.79.rest_0_ = bf16[4096,640]{1,0:T(8,128)(2,1)} custom-call(bf16[4096,5120]{1,0:T(8,128)(2,1)} %du.3.rest_3_.rest_4_.u_ref, bf16[1280,5120]{1,0:T(8,128)(2,1)} %get-tuple-element.27.rest_1_.rest_0_.rest_2_.w_ref, bf16[4096,640]{1,0:T(8,128)(2,1)} %shard_map.77.rest_1_.rest_0_, ...), custom_call_target="tpu_custom_call", output_to_operand_aliasing={{}: (2, {})} | custom-call | flops 6710886400 | bytes 17039360 | tf_op jit(solution)/shard_map/pallas_call | solution.py:372
  530.8 2.4 layer_sum.8
  533.2 0.5 collective-permute-start.13
  533.7 2.5 layer_sum.7
  536.2 1.1 collective-permute-done.8.came_ref
  537.3 0.5 collective-permute-start.11
  537.8 2.5 layer_sum.6
  540.3 24.5 %collective-permute-done.20.came_ref = f32[256,1280]{1,0:T(8,128)S(1)} collective-permute-done((f32[256,1280]{1,0:T(8,128)}, f32[256,1280]{1,0:T(8,128)S(1)}, u32[]{:S(2)}, u32[]{:S(2)}) %collective-permute-start.20) | collective-permute-done | bytes 1310752 | tf_op jit(solution)/shard_map/ppermute | solution.py:571
  564.8 0.5 collective-permute-start.9
  565.3 0.5 copy-done.9
  565.9 3.0 layer_sum.11.refs_2_
  568.9 1.0 collective-permute-start.21
  569.9 19.9 %shard_map.80 = bf16[4096,640]{1,0:T(8,128)(2,1)} custom-call(bf16[4096,5120]{1,0:T(8,128)(2,1)} %du.3.rest_3_.rest_4_.u_ref, bf16[1280,5120]{1,0:T(8,128)(2,1)} %get-tuple-element.27.rest_1_.rest_0_.rest_2_.w_ref, bf16[4096,640]{1,0:T(8,128)(2,1)} %shard_map.79.rest_0_), custom_call_target="tpu_custom_call", output_to_operand_aliasing={{}: (2, {})} | custom-call | flops 13421772800 | bytes 27525120 | tf_op jit(solution)/shard_map/pallas_call | solution.py:372
  589.8 1.4 add.59
  591.2 1.2 add.57
  592.4 5.2 collective-permute-done.11
  597.6 1.2 add.55
  598.8 16.3 %collective-permute-done.9 = f32[320,640]{1,0:T(8,128)} collective-permute-done((f32[320,640]{1,0:T(8,128)}, f32[320,640]{1,0:T(8,128)}, u32[]{:S(2)}, u32[]{:S(2)}) %collective-permute-start.9) | collective-permute-done | bytes 819232 | tf_op jit(solution)/shard_map/ppermute | solution.py:577
  615.1 1.2 add.53
  616.4 2.1 pad_maximum_fusion
  618.5 22.1 %collective-permute-done.21.refs_3_ = f32[256,1280]{1,0:T(8,128)} collective-permute-done((f32[256,1280]{1,0:T(8,128)}, f32[256,1280]{1,0:T(8,128)}, u32[]{:S(2)}, u32[]{:S(2)}) %collective-permute-start.21) | collective-permute-done | bytes 1310752 | tf_op jit(solution)/shard_map/ppermute | solution.py:577
  640.6 1.3 copy-done.8
  641.9 6.4 fin2.1
  (32 shorter events, 0.1 us)
Async XLA Ops:
  116.1 77.3 %collective-permute-start = (bf16[1024,640]{1,0:T(8,128)(2,1)}, bf16[1024,640]{1,0:T(8,128)(2,1)S(1)}, u32[]{:S(2)}, u32[]{:S(2)}) collective-permute-start(bf16[1024,640]{1,0:T(8,128)(2,1)} %get-tuple-element.25), channel_id=1, source_target_pairs={{0,4},{4,0},{1,5},{5,1},{2,6},{6,2},{3,7},{7,3},{8,12},{12,8},{9,1... | collective-permute-start | bytes 3932168 | tf_op jit(solution)/shard_map/ppermute | solution.py:574
  117.5 76.6 %collective-permute-start.1 = (bf16[1024,640]{1,0:T(8,128)(2,1)}, bf16[1024,640]{1,0:T(8,128)(2,1)S(1)}, u32[]{:S(2)}, u32[]{:S(2)}) collective-permute-start(bf16[1024,640]{1,0:T(8,128)(2,1)} %get-tuple-element.26), channel_id=1, source_target_pairs={{0,4},{4,0},{1,5},{5,1},{2,6},{6,2},{3,7},{7,3},{8,12},{12,8},{9,1... | collective-permute-start | bytes 3932168 | tf_op jit(solution)/shard_map/ppermute | solution.py:574
  118.1 206.2 %collective-permute-start.2 = (bf16[1024,640]{1,0:T(8,128)(2,1)}, bf16[1024,640]{1,0:T(8,128)(2,1)}, u32[]{:S(2)}, u32[]{:S(2)}) collective-permute-start(bf16[1024,640]{1,0:T(8,128)(2,1)} %get-tuple-element.33), channel_id=1, source_target_pairs={{0,4},{4,0},{1,5},{5,1},{2,6},{6,2},{3,7},{7,3},{8,12},{12,8},{9,1... | collective-permute-start | bytes 3932168 | tf_op jit(solution)/shard_map/ppermute | solution.py:574
  119.5 204.9 %collective-permute-start.3 = (bf16[1024,640]{1,0:T(8,128)(2,1)}, bf16[1024,640]{1,0:T(8,128)(2,1)}, u32[]{:S(2)}, u32[]{:S(2)}) collective-permute-start(bf16[1024,640]{1,0:T(8,128)(2,1)} %get-tuple-element.34), channel_id=1, source_target_pairs={{0,4},{4,0},{1,5},{5,1},{2,6},{6,2},{3,7},{7,3},{8,12},{12,8},{9,1... | collective-permute-start | bytes 3932168 | tf_op jit(solution)/shard_map/ppermute | solution.py:574
  120.2 167.0 %collective-permute-start.4 = (bf16[1024,640]{1,0:T(8,128)(2,1)}, bf16[1024,640]{1,0:T(8,128)(2,1)}, u32[]{:S(2)}, u32[]{:S(2)}) collective-permute-start(bf16[1024,640]{1,0:T(8,128)(2,1)} %get-tuple-element.36), channel_id=1, source_target_pairs={{0,4},{4,0},{1,5},{5,1},{2,6},{6,2},{3,7},{7,3},{8,12},{12,8},{9,1... | collective-permute-start | bytes 3932168 | tf_op jit(solution)/shard_map/ppermute | solution.py:574
  193.3 1.1 copy-start.2
  193.3 94.6 %collective-permute-start.5 = (bf16[1024,640]{1,0:T(8,128)(2,1)}, bf16[1024,640]{1,0:T(8,128)(2,1)}, u32[]{:S(2)}, u32[]{:S(2)}) collective-permute-start(bf16[1024,640]{1,0:T(8,128)(2,1)} %get-tuple-element.37), channel_id=1, source_target_pairs={{0,4},{4,0},{1,5},{5,1},{2,6},{6,2},{3,7},{7,3},{8,12},{12,8},{9,1... | collective-permute-start | bytes 3932168 | tf_op jit(solution)/shard_map/ppermute | solution.py:574
  194.0 1.2 copy-start.3
  265.1 152.1 %collective-permute-start.17 = (f32[640,1280]{1,0:T(8,128)}, f32[640,1280]{1,0:T(8,128)}, u32[]{:S(2)}, u32[]{:S(2)}) collective-permute-start(f32[640,1280]{1,0:T(8,128)} %get-tuple-element.45), channel_id=1, source_target_pairs={{0,1},{1,0},{2,3},{3,2},{4,5},{5,4},{6,7},{7,6},{8,9},{9,8},{10,11... | collective-permute-start | bytes 9830408 | tf_op jit(solution)/shard_map/ppermute | solution.py:568
  384.3 38.2 %collective-permute-start.7 = (f32[320,2560]{1,0:T(8,128)}, f32[320,2560]{1,0:T(8,128)}, u32[]{:S(2)}, u32[]{:S(2)}) collective-permute-start(f32[320,2560]{1,0:T(8,128)} %get-tuple-element.43), channel_id=1, source_target_pairs={{0,1},{1,0},{2,3},{3,2},{4,5},{5,4},{6,7},{7,6},{8,9},{9,8},{10,11... | collective-permute-start | bytes 9830408 | tf_op jit(solution)/shard_map/ppermute | solution.py:568
  416.5 6.0 copy-start.1
  416.5 23.3 %collective-permute-start.6 = (f32[320,2560]{1,0:T(8,128)}, f32[320,2560]{1,0:T(8,128)S(1)}, u32[]{:S(2)}, u32[]{:S(2)}) collective-permute-start(f32[320,2560]{1,0:T(8,128)} %get-tuple-element.42), channel_id=1, source_target_pairs={{0,1},{1,0},{2,3},{3,2},{4,5},{5,4},{6,7},{7,6},{8,9},{9,8},{10,11... | collective-permute-start | bytes 9830408 | tf_op jit(solution)/shard_map/ppermute | solution.py:568
  417.1 71.3 %collective-permute-start.16 = (f32[640,1280]{1,0:T(8,128)}, f32[640,1280]{1,0:T(8,128)}, u32[]{:S(2)}, u32[]{:S(2)}) collective-permute-start(f32[640,1280]{1,0:T(8,128)} %get-tuple-element.44), channel_id=1, source_target_pairs={{0,1},{1,0},{2,3},{3,2},{4,5},{5,4},{6,7},{7,6},{8,9},{9,8},{10,11... | collective-permute-start | bytes 9830408 | tf_op jit(solution)/shard_map/ppermute | solution.py:568
  421.1 68.1 %collective-permute-start.18 = (f32[384,1280]{1,0:T(8,128)}, f32[384,1280]{1,0:T(8,128)}, u32[]{:S(2)}, u32[]{:S(2)}) collective-permute-start(f32[384,1280]{1,0:T(8,128)} %slice_add_fusion), channel_id=1, source_target_pairs={{0,2},{1,3},{2,0},{3,1},{4,6},{5,7},{6,4},{7,5},{8,10},{9,11},{10,... | collective-permute-start | bytes 5898248 | tf_op jit(solution)/shard_map/ppermute | solution.py:571
  425.9 58.7 %collective-permute-start.14 = (f32[320,640]{1,0:T(8,128)}, f32[320,640]{1,0:T(8,128)}, u32[]{:S(2)}, u32[]{:S(2)}) collective-permute-start(f32[320,640]{1,0:T(8,128)} %get-tuple-element.47), channel_id=1, source_target_pairs={{0,2},{1,3},{2,0},{3,1},{4,6},{5,7},{6,4},{7,5},{8,10},{9,11},{10,... | collective-permute-start | bytes 2457608 | tf_op jit(solution)/shard_map/ppermute | solution.py:571
  435.5 80.9 %collective-permute-start.12 = (f32[320,640]{1,0:T(8,128)}, f32[320,640]{1,0:T(8,128)}, u32[]{:S(2)}, u32[]{:S(2)}) collective-permute-start(f32[320,640]{1,0:T(8,128)} %get-tuple-element.48), channel_id=1, source_target_pairs={{0,2},{1,3},{2,0},{3,1},{4,6},{5,7},{6,4},{7,5},{8,10},{9,11},{10,... | collective-permute-start | bytes 2457608 | tf_op jit(solution)/shard_map/ppermute | solution.py:571
  439.8 46.2 %copy-start = (f32[320,2560]{1,0:T(8,128)}, f32[320,2560]{1,0:T(8,128)S(1)}, u32[]{:S(2)}) copy-start(f32[320,2560]{1,0:T(8,128)S(1)} %collective-permute-done.6.got_ref) | copy-start | bytes 9830404
  439.8 93.4 %collective-permute-start.10 = (f32[320,640]{1,0:T(8,128)}, f32[320,640]{1,0:T(8,128)}, u32[]{:S(2)}, u32[]{:S(2)}) collective-permute-start(f32[320,640]{1,0:T(8,128)} %get-tuple-element.49), channel_id=1, source_target_pairs={{0,2},{1,3},{2,0},{3,1},{4,6},{5,7},{6,4},{7,5},{8,10},{9,11},{10,... | collective-permute-start | bytes 2457608 | tf_op jit(solution)/shard_map/ppermute | solution.py:571
  484.6 52.7 %collective-permute-start.8 = (f32[320,640]{1,0:T(8,128)S(1)}, f32[320,640]{1,0:T(8,128)}, u32[]{:S(2)}, u32[]{:S(2)}) collective-permute-start(f32[320,640]{1,0:T(8,128)S(1)} %get-tuple-element.46), channel_id=1, source_target_pairs={{0,2},{1,3},{2,0},{3,1},{4,6},{5,7},{6,4},{7,5},{8,10},{9,11},{10,... | collective-permute-start | bytes 2457608 | tf_op jit(solution)/shard_map/ppermute | solution.py:571
  488.4 76.4 %collective-permute-start.20 = (f32[256,1280]{1,0:T(8,128)}, f32[256,1280]{1,0:T(8,128)S(1)}, u32[]{:S(2)}, u32[]{:S(2)}) collective-permute-start(f32[256,1280]{1,0:T(8,128)} %slice_add_fusion.1), channel_id=1, source_target_pairs={{0,2},{1,3},{2,0},{3,1},{4,6},{5,7},{6,4},{7,5},{8,10},{9,11},{10,... | collective-permute-start | bytes 3932168 | tf_op jit(solution)/shard_map/ppermute | solution.py:571
  489.1 79.8 %collective-permute-start.15 = (f32[320,640]{1,0:T(8,128)}, f32[320,640]{1,0:T(8,128)}, u32[]{:S(2)}, u32[]{:S(2)}) collective-permute-start(f32[320,640]{1,0:T(8,128)} %layer_sum.9), channel_id=1, source_target_pairs={{0,8},{8,0},{1,9},{9,1},{2,10},{10,2},{3,11},{11,3},{4,12},{12,4},... | collective-permute-start | bytes 2457608 | tf_op jit(solution)/shard_map/ppermute | solution.py:577
  516.5 124.1 %collective-permute-start.19 = (f32[384,1280]{1,0:T(8,128)}, f32[384,1280]{1,0:T(8,128)S(1)}, u32[]{:S(2)}, u32[]{:S(2)}) collective-permute-start(f32[384,1280]{1,0:T(8,128)} %layer_sum.10.refs_0_), channel_id=1, source_target_pairs={{0,8},{8,0},{1,9},{9,1},{2,10},{10,2},{3,11},{11,3},{4,12},{12,4},... | collective-permute-start | bytes 5898248 | tf_op jit(solution)/shard_map/ppermute | solution.py:577
  533.2 58.0 %collective-permute-start.13 = (f32[320,640]{1,0:T(8,128)}, f32[320,640]{1,0:T(8,128)}, u32[]{:S(2)}, u32[]{:S(2)}) collective-permute-start(f32[320,640]{1,0:T(8,128)} %layer_sum.8), channel_id=1, source_target_pairs={{0,8},{8,0},{1,9},{9,1},{2,10},{10,2},{3,11},{11,3},{4,12},{12,4},... | collective-permute-start | bytes 2457608 | tf_op jit(solution)/shard_map/ppermute | solution.py:577
  537.3 60.3 %collective-permute-start.11 = (f32[320,640]{1,0:T(8,128)}, f32[320,640]{1,0:T(8,128)}, u32[]{:S(2)}, u32[]{:S(2)}) collective-permute-start(f32[320,640]{1,0:T(8,128)} %layer_sum.7), channel_id=1, source_target_pairs={{0,8},{8,0},{1,9},{9,1},{2,10},{10,2},{3,11},{11,3},{4,12},{12,4},... | collective-permute-start | bytes 2457608 | tf_op jit(solution)/shard_map/ppermute | solution.py:577
  564.8 1.1 copy-start.9
  564.8 50.3 %collective-permute-start.9 = (f32[320,640]{1,0:T(8,128)}, f32[320,640]{1,0:T(8,128)}, u32[]{:S(2)}, u32[]{:S(2)}) collective-permute-start(f32[320,640]{1,0:T(8,128)} %layer_sum.6), channel_id=1, source_target_pairs={{0,8},{8,0},{1,9},{9,1},{2,10},{10,2},{3,11},{11,3},{4,12},{12,4},... | collective-permute-start | bytes 2457608 | tf_op jit(solution)/shard_map/ppermute | solution.py:577
  568.9 20.9 %copy-start.4 = (f32[320,640]{1,0:T(8,128)S(1)}, f32[320,640]{1,0:T(8,128)}, u32[]{:S(2)}) copy-start(f32[320,640]{1,0:T(8,128)} %layer_sum.9) | copy-start | bytes 2457604
  568.9 22.3 %copy-start.5 = (f32[320,640]{1,0:T(8,128)S(1)}, f32[320,640]{1,0:T(8,128)}, u32[]{:S(2)}) copy-start(f32[320,640]{1,0:T(8,128)} %layer_sum.8) | copy-start | bytes 2457604
  568.9 71.7 %collective-permute-start.21 = (f32[256,1280]{1,0:T(8,128)}, f32[256,1280]{1,0:T(8,128)}, u32[]{:S(2)}, u32[]{:S(2)}) collective-permute-start(f32[256,1280]{1,0:T(8,128)} %layer_sum.11.refs_2_), channel_id=1, source_target_pairs={{0,8},{8,0},{1,9},{9,1},{2,10},{10,2},{3,11},{11,3},{4,12},{12,4},... | collective-permute-start | bytes 3932168 | tf_op jit(solution)/shard_map/ppermute | solution.py:577
  589.8 7.8 %copy-start.6 = (f32[320,640]{1,0:T(8,128)S(1)}, f32[320,640]{1,0:T(8,128)}, u32[]{:S(2)}) copy-start(f32[320,640]{1,0:T(8,128)} %layer_sum.7) | copy-start | bytes 2457604
  589.8 25.3 %copy-start.7 = (f32[320,640]{1,0:T(8,128)S(1)}, f32[320,640]{1,0:T(8,128)}, u32[]{:S(2)}) copy-start(f32[320,640]{1,0:T(8,128)} %layer_sum.6) | copy-start | bytes 2457604
  640.6 1.3 copy-start.8
where the time goes:
time: 657 us; the launch traced here: 649 us
  Pallas kernels  494 us (75%)
  waiting for transfers between devices  114 us (17%)
  other arithmetic  18.7 us (3%)
  starting transfers between devices  17.6 us (3%)
    pallas_call x1, Pallas kernels, gather_kernel(): pl.pallas_call(gather_body, in_specs=[pl.BlockSpec(memory_space=pl.ANY)]...  115 us
    pallas_call x2, Pallas kernels, up_kernel(): pl.pallas_call(make_up_body(call * PER * rows, len(x_oth)), grid=(f // bn...  96.8 us
    pallas_call x6, Pallas kernels, out_kernel(): pl.pallas_call(body, grid=(count,), in_specs=[pl.BlockSpec((bm, f), lambd...  94.8 us
    pallas_call x2, Pallas kernels, du_kernel(): pl.pallas_call(make_du_body(call * PER * rows, len(g_oth)), grid=(f // bn...  72.9 us
    ppermute x6, waiting for transfers between devices, over_x(): return lax.ppermute(v, 'row', x_pair)  69.9 us
    pallas_call x2, Pallas kernels, dw1_kernel(): pl.pallas_call(dw1_body, grid_spec=pltpu.PrefetchScalarGridSpec(num_scala...  46.6 us
    ppermute x6, waiting for transfers between devices, over_depth(): return lax.ppermute(v, 'depth', pair)  43.5 us
    pallas_call x2, Pallas kernels, dw2_kernel(): pl.pallas_call(dw2_body, grid_spec=pltpu.PrefetchScalarGridSpec(num_scala...  43.5 us
  transfers between devices with their start and end apart: 22, of which 7 were waited for; matrix products, arithmetic and copies ran while one was open for 3% of the time, Pallas kernels for 57%

commit v1 on v0

--- a/solution.py
+++ b/solution.py
@@ -15,7 +15,7 @@
 NPIECE1 = 4
 PER = 2
 NSLOT = 3
-PIECE = 256
+PIECE = 128
 TILE = 16
 SUB = 512
 MESH = pl.DeviceIdType.MESH
@@ -213,9 +213,10 @@
                 u2 = u * u
                 t = jnp.tanh(u * (SQRT_2_OVER_PI + (SQRT_2_OVER_PI * CUBIC) * u2))
                 h = 0.5 + 0.5 * t
-                a_ref[slot, sl, :] = (u * h).astype(BF16)
-                slope = 0.5 * SQRT_2_OVER_PI + (1.5 * SQRT_2_OVER_PI * CUBIC) * u2
-                d_ref[slot, sl, :] = h + ((1.0 - t * t) * u) * slope
+                act = u * h
+                a_ref[slot, sl, :] = act.astype(BF16)
+                slope = 2.0 * SQRT_2_OVER_PI + (6.0 * SQRT_2_OVER_PI * CUBIC) * u2
+                d_ref[slot, sl, :] = h + (h * (u - act)) * slope
 
         @pl.when(j == 0)
         def _():
@@ -590,7 +591,7 @@
         grad_oth = [over_col(cut[nlater + i]) for i in range(NCHUNK)]
 
         outs = {"y": None, "dx": None}
-        parts = {"y": ((0, 4), (4, 4)), "dx": ((0, 1), (1, 1), (2, 2), (4, 4))}
+        parts = {"y": ((0, 4), (4, 2), (6, 2)), "dx": ((0, 1), (1, 3), (4, 4))}
 
         def out_part(key, part, after=None):
             args = (y_body, "y", a, w2, (w2.shape[0], hh)) if key == "y" else (dx_body, "dx", du, w1, (hh, w1.shape[1]))
@@ -606,7 +607,7 @@
         got_away = over_core(away[1])
         got_here = over_core(here[1])
         pieces, at = [], 0
-        for n in (384, hh - 384):
+        for n in (256, hh - 256):
             came = over_x(away[0][at:at + n] + got_away[at:at + n])
             layer = sum_kernel(here[0], got_here, came, lambda i, at=at: (at // 128 + i, 0), n // 128)
             pieces.append((layer, over_depth(layer)))
@@ -618,8 +619,7 @@
             du = du_kernel(grad, grad_oth[i * PER:(i + 1) * PER], w2, d, rows, i, du, here[0])
 
         away = dw1_kernel(jnp.stack([(1 - x + col) % 2, col, core]), tok, (tok_first, *tok_later), du, fh, du)
-        dep = out_part("dx", 0, away[0])
-        here = dw1_kernel(jnp.stack([(x + col) % 2, col, core]), tok, (tok_first, *tok_later), du, fh, dep)
+        here = dw1_kernel(jnp.stack([(x + col) % 2, col, core]), tok, (tok_first, *tok_later), du, fh, away[0])
         got_away = over_core(away[1])
         got_here = over_core(here[1])
         cols = []
@@ -632,10 +632,11 @@
             cols.append(layer + over_depth(layer))
         dw_up = jnp.concatenate(cols, axis=1)
 
-        out_part("dx", 1, here[0])
+        out_part("dx", 0, here[0])
         out_part("y", 1, outs["dx"])
-        out_part("dx", 2, outs["y"])
-        out_part("dx", 3)
+        out_part("y", 2)
+        out_part("dx", 1, outs["y"])
+        out_part("dx", 2)
         return outs["y"], outs["dx"], dw_up, dw_down
 
     return jax.shard_map(body, mesh=mesh, in_specs=(act_spec, weight_spec, weight_spec, act_spec),

time: 657 us -> 650 us (0.989)
  waiting for transfers between devices: 114 us -> 107 us
    ppermute x6, waiting for transfers between devices: 43.5 us -> 30.4 us  [over_depth(): return lax.ppermute(v, 'depth', pair)]
  transfers between devices with their start and end apart: 22 -> 22, of which waited for: 7 -> 7; matrix products, arithmetic and copies ran while one was open for 3% -> 3% of each run, Pallas kernels for 57% -> 58%
where the time goes in v1:
time: 650 us; the launch traced here: 639 us
  Pallas kernels  491 us (76%)
  waiting for transfers between devices  107 us (16%)
  other arithmetic  19.4 us (3%)
  starting transfers between devices  17.1 us (3%)
    pallas_call x1, Pallas kernels, gather_kernel(): pl.pallas_call(gather_body, in_specs=[pl.BlockSpec(memory_space=pl.ANY)]...  115 us
    pallas_call x6, Pallas kernels, out_kernel(): pl.pallas_call(body, grid=(count,), in_specs=[pl.BlockSpec((bm, f), lambd...  94.4 us
    pallas_call x2, Pallas kernels, up_kernel(): pl.pallas_call(make_up_body(call * PER * rows, len(x_oth)), grid=(f // bn...  94.4 us
    pallas_call x2, Pallas kernels, du_kernel(): pl.pallas_call(make_du_body(call * PER * rows, len(g_oth)), grid=(f // bn...  73.3 us
    ppermute x6, waiting for transfers between devices, over_x(): return lax.ppermute(v, 'row', x_pair)  73.1 us
    pallas_call x2, Pallas kernels, dw1_kernel(): pl.pallas_call(dw1_body, grid_spec=pltpu.PrefetchScalarGridSpec(num_scala...  46.6 us
    pallas_call x2, Pallas kernels, dw2_kernel(): pl.pallas_call(dw2_body, grid_spec=pltpu.PrefetchScalarGridSpec(num_scala...  43 us
    ppermute x6, waiting for transfers between devices, over_depth(): return lax.ppermute(v, 'depth', pair)  30.4 us
  transfers between devices with their start and end apart: 22, of which 7 were waited for; matrix products, arithmetic and copies ran while one was open for 3% of the time, Pallas kernels for 58%

profile of v1, /device:TPU:0, one launch (start us, length us, event | category | flops | bytes accessed | tf_op | source)
XLA Modules:
  0.0 639.2 jit_solution(14862979222832677084)
XLA Ops:
  0.6 115.4 %gather.1 = (bf16[1280,5120]{1,0:T(8,128)(2,1)}, bf16[5120,1280]{1,0:T(8,128)(2,1)}, bf16[2048,640]{1,0:T(8,128)(2,1)}, bf16[1024,640]{1,0:T(8,128)(2,1)}, bf16[...) custom-call(bf16[320,2560]{1,0:T(8,128)(2,1)} %w1_ref.1, ...), custom_call_target="tpu_custom_call" | custom-call | bytes 300000000 | tf_op jit(solution)/shard_map/gather/pallas_call | solution.py:161
  116.1 1.4 collective-permute-start
  117.5 0.7 collective-permute-start.1
  118.1 1.4 collective-permute-start.2
  119.5 0.7 collective-permute-start.3
  120.2 1.4 collective-permute-start.4
  121.5 47.2 %up.2 = (bf16[4096,5120]{1,0:T(8,128)(2,1)}, f32[4096,5120]{1,0:T(8,128)}) custom-call(bf16[4096,640]{1,0:T(8,128)(2,1)} %own_ref.3, bf16[2048,640]{1,0:T(8,128)(2,1)} %get-tuple-element.28.rest_0_, bf16[1280,5120]{1,0:T(8,128)(2,1)} %get-tuple-element.27.rest_1_.rest_0_.rest_2_.w_ref), custom_call_target="tpu_custom_call" | custom-call | flops 26843545600 | bytes 76021760 | tf_op jit(solution)/shard_map/up/pallas_call | solution.py:275
  168.8 0.6 pad_add_fusion
  169.4 0.7 add_add_fusion
  170.0 22.1 %shard_map.75.rest_5_.rest_0_ = bf16[4096,640]{1,0:T(8,128)(2,1)} custom-call(bf16[4096,5120]{1,0:T(8,128)(2,1)} %get-tuple-element.29.a_ref.rest_3_, bf16[5120,1280]{1,0:T(8,128)(2,1)} %get-tuple-element.31.w_ref.rest_2_, bf16[1280,5120]{1,0:T(8,128)(2,1)} %get-tuple-element.27.rest_1_.rest_0_.rest_2_.w_ref), custom_call_target="tpu_custom_call" | custom-call | flops 13421772800 | bytes 27525120 | tf_op jit(solution)/shard_map/pallas_call | solution.py:373
  192.2 0.6 collective-permute-start.5
  192.8 0.4 copy-done.1
  193.2 0.7 copy-done.2
  193.9 47.1 %up.3 = (bf16[4096,5120]{1,0:T(8,128)(2,1)}, f32[4096,5120]{1,0:T(8,128)}) custom-call(bf16[4096,640]{1,0:T(8,128)(2,1)} %own_ref.3, bf16[1024,640]{1,0:T(8,128)(2,1)} %copy-done.1, bf16[1024,640]{1,0:T(8,128)(2,1)} %copy-done.2, bf16[1280,5120]{1,0:T(8,128)(2,1)} %get-tuple-element.27.rest_1_.rest_0_.rest_2_.w_ref, ...), custom_call_target="tpu_custom_call", output_to_operand_aliasing={{0}: (4, {}), {1}: (5, {})} | custom-call | flops 26843545600 | bytes 76021760 | tf_op jit(solution)/shard_map/up/pallas_call | solution.py:275
  241.0 21.5 %dw2.2 = (f32[640,1280]{1,0:T(8,128)}, f32[640,1280]{1,0:T(8,128)}) custom-call(s32[2]{0:T(128)} %get-tuple-element.51.s_ref, bf16[4096,640]{1,0:T(8,128)(2,1)} %go_ref.3, bf16[4096,5120]{1,0:T(8,128)(2,1)} %get-tuple-element.32.a_ref, f32[4096,5120]{1,0:T(8,128)} %get-tuple-element.35.dep_ref.rest_3_), custom_call_target="tpu_custom_call" | custom-call | flops 13421772800 | bytes 32768000 | tf_op jit(solution)/shard_map/dw2/pallas_call | solution.py:438
  262.6 21.5 %dw2.3 = (f32[640,1280]{1,0:T(8,128)}, f32[640,1280]{1,0:T(8,128)}) custom-call(s32[2]{0:T(128)} %get-tuple-element.50.s_ref, bf16[4096,640]{1,0:T(8,128)(2,1)} %go_ref.3, bf16[4096,5120]{1,0:T(8,128)(2,1)} %get-tuple-element.32.a_ref, f32[640,1280]{1,0:T(8,128)} %get-tuple-element.38.dep_ref), custom_call_target="tpu_custom_call" | custom-call | flops 13421772800 | bytes 32768000 | tf_op jit(solution)/shard_map/dw2/pallas_call | solution.py:438
  284.1 3.8 collective-permute-done.5.rest_1_
  288.0 36.9 %du.2.rest_4_ = bf16[4096,5120]{1,0:T(8,128)(2,1)} custom-call(bf16[4096,640]{1,0:T(8,128)(2,1)} %go_ref.3, bf16[1024,640]{1,0:T(8,128)(2,1)} %collective-permute-done.4.rest_0_, bf16[1024,640]{1,0:T(8,128)(2,1)} %collective-permute-done.5.rest_1_, bf16[5120,1280]{1,0:T(8,128)(2,1)} %get-tuple-element.31.w_ref.rest_2_, ...), custom_call_target="tpu_custom_call" | custom-call | flops 26843545600 | bytes 76021760 | tf_op jit(solution)/shard_map/du/pallas_call | solution.py:345
  324.9 36.4 %du.3.rest_3_.rest_4_.u_ref = bf16[4096,5120]{1,0:T(8,128)(2,1)} custom-call(bf16[4096,640]{1,0:T(8,128)(2,1)} %go_ref.3, bf16[1024,640]{1,0:T(8,128)(2,1)} %collective-permute-done.2.rest_0_, bf16[1024,640]{1,0:T(8,128)(2,1)} %collective-permute-done.3.rest_1_, bf16[5120,1280]{1,0:T(8,128)(2,1)} %get-tuple-element.31.w_ref.rest_2_, ...), custom_call_target="tpu_custom_call", output_to_operand_aliasing={{}: (5, {})} | custom-call | flops 26843545600 | bytes 76021760 | tf_op jit(solution)/shard_map/du/pallas_call | solution.py:345
  361.3 23.2 %dw1.2 = (f32[320,2560]{1,0:T(8,128)}, f32[320,2560]{1,0:T(8,128)}) custom-call(s32[3]{0:T(128)} %get-tuple-element.53.s_ref, bf16[4096,640]{1,0:T(8,128)(2,1)} %own_ref.3, bf16[2048,640]{1,0:T(8,128)(2,1)} %get-tuple-element.28.rest_0_, bf16[1024,640]{1,0:T(8,128)(2,1)} %copy-done.1, bf16[1024,640]{1,0:T(8,128)(2,1)} %copy-done.2, ...), custom_call_target="tpu_custom_call" | custom-call | flops 13421772800 | bytes 32768000 | tf_op jit(solution)/shard_map/dw1/pallas_call | solution.py:500
  384.6 23.4 %dw1.3 = (f32[320,2560]{1,0:T(8,128)}, f32[320,2560]{1,0:T(8,128)}) custom-call(s32[3]{0:T(128)} %get-tuple-element.52.s_ref, bf16[4096,640]{1,0:T(8,128)(2,1)} %own_ref.3, bf16[2048,640]{1,0:T(8,128)(2,1)} %get-tuple-element.28.rest_0_, bf16[1024,640]{1,0:T(8,128)(2,1)} %copy-done.1, bf16[1024,640]{1,0:T(8,128)(2,1)} %copy-done.2, ...), custom_call_target="tpu_custom_call" | custom-call | flops 13421772800 | bytes 32768000 | tf_op jit(solution)/shard_map/dw1/pallas_call | solution.py:500
  408.0 0.7 collective-permute-start.6
  408.6 0.0 collective-permute-start.16
  408.7 8.9 %shard_map.76.rest_1_.rest_0_ = bf16[4096,640]{1,0:T(8,128)(2,1)} custom-call(bf16[4096,5120]{1,0:T(8,128)(2,1)} %du.3.rest_3_.rest_4_.u_ref, bf16[1280,5120]{1,0:T(8,128)(2,1)} %get-tuple-element.27.rest_1_.rest_0_.rest_2_.w_ref, f32[320,2560]{1,0:T(8,128)} %get-tuple-element.41.rest_0_.here_ref), custom_call_target="tpu_custom_call" | custom-call | flops 3355443200 | bytes 11796480 | tf_op jit(solution)/shard_map/pallas_call | solution.py:373
  417.6 3.6 slice_add_fusion
  421.2 1.3 collective-permute-start.20
  422.6 13.3 %shard_map.77.rest_0_ = bf16[4096,640]{1,0:T(8,128)(2,1)} custom-call(bf16[4096,5120]{1,0:T(8,128)(2,1)} %get-tuple-element.32.a_ref, bf16[5120,1280]{1,0:T(8,128)(2,1)} %get-tuple-element.31.w_ref.rest_2_, bf16[4096,640]{1,0:T(8,128)(2,1)} %shard_map.75.rest_5_.rest_0_, bf16[4096,640]{1,0:T(8,128)(2,1)} %shard_map.76.rest_1_.rest_0_), custom_call_target="tpu_custom_call", output_to_operand_aliasing={{}: (2, {})} | custom-call | flops 6710886400 | bytes 17039360 | tf_op jit(solution)/shard_map/pallas_call | solution.py:373
  435.9 4.4 slice_add_fusion.5
  440.3 0.7 collective-permute-start.14
  441.0 1.3 collective-permute-start.12
  442.3 2.9 slice_add_fusion.1
  445.3 0.7 collective-permute-start.18
  445.9 13.7 %shard_map.78.rest_1_ = bf16[4096,640]{1,0:T(8,128)(2,1)} custom-call(bf16[4096,5120]{1,0:T(8,128)(2,1)} %get-tuple-element.32.a_ref, bf16[5120,1280]{1,0:T(8,128)(2,1)} %get-tuple-element.31.w_ref.rest_2_, bf16[4096,640]{1,0:T(8,128)(2,1)} %shard_map.77.rest_0_), custom_call_target="tpu_custom_call", output_to_operand_aliasing={{}: (2, {})} | custom-call | flops 6710886400 | bytes 17039360 | tf_op jit(solution)/shard_map/pallas_call | solution.py:373
  459.6 25.2 %collective-permute-done.14.came_ref = f32[320,640]{1,0:T(8,128)} collective-permute-done((f32[320,640]{1,0:T(8,128)}, f32[320,640]{1,0:T(8,128)}, u32[]{:S(2)}, u32[]{:S(2)}) %collective-permute-start.14) | collective-permute-done | bytes 819232 | tf_op jit(solution)/shard_map/ppermute | solution.py:572
  484.8 1.3 collective-permute-start.10
  486.1 2.5 layer_sum.9
  488.6 0.7 collective-permute-start.8
  489.3 0.5 collective-permute-start.15
  489.8 4.6 layer_sum.11.refs_2_
  494.5 7.9 %collective-permute-done.12.came_ref = f32[320,640]{1,0:T(8,128)} collective-permute-done((f32[320,640]{1,0:T(8,128)S(1)}, f32[320,640]{1,0:T(8,128)}, u32[]{:S(2)}, u32[]{:S(2)}) %collective-permute-start.12) | collective-permute-done | bytes 819232 | tf_op jit(solution)/shard_map/ppermute | solution.py:572
  502.4 0.5 collective-permute-start.21
  502.9 16.2 %shard_map.79.rest_0_ = bf16[4096,640]{1,0:T(8,128)(2,1)} custom-call(bf16[4096,5120]{1,0:T(8,128)(2,1)} %du.3.rest_3_.rest_4_.u_ref, bf16[1280,5120]{1,0:T(8,128)(2,1)} %get-tuple-element.27.rest_1_.rest_0_.rest_2_.w_ref, bf16[4096,640]{1,0:T(8,128)(2,1)} %shard_map.76.rest_1_.rest_0_, ...), custom_call_target="tpu_custom_call", output_to_operand_aliasing={{}: (2, {})} | custom-call | flops 10066329600 | bytes 22282240 | tf_op jit(solution)/shard_map/pallas_call | solution.py:373
  519.1 2.4 layer_sum.8
  521.6 26.3 %collective-permute-done.10.came_ref = f32[320,640]{1,0:T(8,128)S(1)} collective-permute-done((f32[320,640]{1,0:T(8,128)}, f32[320,640]{1,0:T(8,128)S(1)}, u32[]{:S(2)}, u32[]{:S(2)}) %collective-permute-start.10) | collective-permute-done | bytes 819232 | tf_op jit(solution)/shard_map/ppermute | solution.py:572
  547.9 0.5 collective-permute-start.13
  548.4 0.4 copy-done.9
  548.8 2.5 layer_sum.7
  551.3 13.7 %collective-permute-done.8.came_ref = f32[320,640]{1,0:T(8,128)S(1)} collective-permute-done((f32[320,640]{1,0:T(8,128)}, f32[320,640]{1,0:T(8,128)S(1)}, u32[]{:S(2)}, u32[]{:S(2)}) %collective-permute-start.8) | collective-permute-done | bytes 819232 | tf_op jit(solution)/shard_map/ppermute | solution.py:572
  564.9 0.5 collective-permute-start.11
  565.5 0.4 copy-done.8
  565.9 2.5 layer_sum.6
  568.4 1.1 collective-permute-start.9
  569.4 3.0 layer_sum.10.refs_0_
  572.5 1.0 collective-permute-start.19
  573.4 20.1 %shard_map.80 = bf16[4096,640]{1,0:T(8,128)(2,1)} custom-call(bf16[4096,5120]{1,0:T(8,128)(2,1)} %du.3.rest_3_.rest_4_.u_ref, bf16[1280,5120]{1,0:T(8,128)(2,1)} %get-tuple-element.27.rest_1_.rest_0_.rest_2_.w_ref, bf16[4096,640]{1,0:T(8,128)(2,1)} %shard_map.79.rest_0_), custom_call_target="tpu_custom_call", output_to_operand_aliasing={{}: (2, {})} | custom-call | flops 13421772800 | bytes 27525120 | tf_op jit(solution)/shard_map/pallas_call | solution.py:373
  593.6 1.4 add.59
  594.9 1.2 add.57
  596.2 1.2 add.55
  597.4 6.5 %collective-permute-done.9 = f32[320,640]{1,0:T(8,128)} collective-permute-done((f32[320,640]{1,0:T(8,128)}, f32[320,640]{1,0:T(8,128)}, u32[]{:S(2)}, u32[]{:S(2)}) %collective-permute-start.9) | collective-permute-done | bytes 819232 | tf_op jit(solution)/shard_map/ppermute | solution.py:578
  603.9 1.2 add.53
  605.2 2.1 pad_maximum_fusion
  607.3 23.9 %collective-permute-done.19.refs_1_ = f32[256,1280]{1,0:T(8,128)} collective-permute-done((f32[256,1280]{1,0:T(8,128)}, f32[256,1280]{1,0:T(8,128)}, u32[]{:S(2)}, u32[]{:S(2)}) %collective-permute-start.19) | collective-permute-done | bytes 1310752 | tf_op jit(solution)/shard_map/ppermute | solution.py:578
  631.2 1.3 copy-done.7
  632.5 6.4 %fin2.1 = f32[1280,640]{1,0:T(8,128)} custom-call(f32[256,1280]{1,0:T(8,128)} %layer_sum.10.refs_0_, f32[256,1280]{1,0:T(8,128)} %collective-permute-done.19.refs_1_, f32[384,1280]{1,0:T(8,128)} %layer_sum.11.refs_2_, f32[384,1280]{1,0:T(8,128)} %copy-done.7), custom_call_target="tpu_custom_call" | custom-call | flops 819200 | bytes 9830400 | tf_op jit(solution)/shard_map/fin2/pallas_call | solution.py:548
  (32 shorter events, 0.2 us)
Async XLA Ops:
  116.1 76.1 %collective-permute-start = (bf16[1024,640]{1,0:T(8,128)(2,1)}, bf16[1024,640]{1,0:T(8,128)(2,1)S(1)}, u32[]{:S(2)}, u32[]{:S(2)}) collective-permute-start(bf16[1024,640]{1,0:T(8,128)(2,1)} %get-tuple-element.25), channel_id=1, source_target_pairs={{0,4},{4,0},{1,5},{5,1},{2,6},{6,2},{3,7},{7,3},{8,12},{12,8},{9,1... | collective-permute-start | bytes 3932168 | tf_op jit(solution)/shard_map/ppermute | solution.py:575
  117.5 75.3 %collective-permute-start.1 = (bf16[1024,640]{1,0:T(8,128)(2,1)}, bf16[1024,640]{1,0:T(8,128)(2,1)S(1)}, u32[]{:S(2)}, u32[]{:S(2)}) collective-permute-start(bf16[1024,640]{1,0:T(8,128)(2,1)} %get-tuple-element.26), channel_id=1, source_target_pairs={{0,4},{4,0},{1,5},{5,1},{2,6},{6,2},{3,7},{7,3},{8,12},{12,8},{9,1... | collective-permute-start | bytes 3932168 | tf_op jit(solution)/shard_map/ppermute | solution.py:575
  118.1 206.7 %collective-permute-start.2 = (bf16[1024,640]{1,0:T(8,128)(2,1)}, bf16[1024,640]{1,0:T(8,128)(2,1)}, u32[]{:S(2)}, u32[]{:S(2)}) collective-permute-start(bf16[1024,640]{1,0:T(8,128)(2,1)} %get-tuple-element.33), channel_id=1, source_target_pairs={{0,4},{4,0},{1,5},{5,1},{2,6},{6,2},{3,7},{7,3},{8,12},{12,8},{9,1... | collective-permute-start | bytes 3932168 | tf_op jit(solution)/shard_map/ppermute | solution.py:575
  119.5 205.3 %collective-permute-start.3 = (bf16[1024,640]{1,0:T(8,128)(2,1)}, bf16[1024,640]{1,0:T(8,128)(2,1)}, u32[]{:S(2)}, u32[]{:S(2)}) collective-permute-start(bf16[1024,640]{1,0:T(8,128)(2,1)} %get-tuple-element.34), channel_id=1, source_target_pairs={{0,4},{4,0},{1,5},{5,1},{2,6},{6,2},{3,7},{7,3},{8,12},{12,8},{9,1... | collective-permute-start | bytes 3932168 | tf_op jit(solution)/shard_map/ppermute | solution.py:575
  120.2 164.0 %collective-permute-start.4 = (bf16[1024,640]{1,0:T(8,128)(2,1)}, bf16[1024,640]{1,0:T(8,128)(2,1)}, u32[]{:S(2)}, u32[]{:S(2)}) collective-permute-start(bf16[1024,640]{1,0:T(8,128)(2,1)} %get-tuple-element.36), channel_id=1, source_target_pairs={{0,4},{4,0},{1,5},{5,1},{2,6},{6,2},{3,7},{7,3},{8,12},{12,8},{9,1... | collective-permute-start | bytes 3932168 | tf_op jit(solution)/shard_map/ppermute | solution.py:575
  192.2 1.1 copy-start.1
  192.2 95.8 %collective-permute-start.5 = (bf16[1024,640]{1,0:T(8,128)(2,1)}, bf16[1024,640]{1,0:T(8,128)(2,1)}, u32[]{:S(2)}, u32[]{:S(2)}) collective-permute-start(bf16[1024,640]{1,0:T(8,128)(2,1)} %get-tuple-element.37), channel_id=1, source_target_pairs={{0,4},{4,0},{1,5},{5,1},{2,6},{6,2},{3,7},{7,3},{8,12},{12,8},{9,1... | collective-permute-start | bytes 3932168 | tf_op jit(solution)/shard_map/ppermute | solution.py:575
  192.8 1.1 copy-start.2
  262.5 155.1 %collective-permute-start.17 = (f32[640,1280]{1,0:T(8,128)}, f32[640,1280]{1,0:T(8,128)}, u32[]{:S(2)}, u32[]{:S(2)}) collective-permute-start(f32[640,1280]{1,0:T(8,128)} %get-tuple-element.45), channel_id=1, source_target_pairs={{0,1},{1,0},{2,3},{3,2},{4,5},{5,4},{6,7},{7,6},{8,9},{9,8},{10,11... | collective-permute-start | bytes 9830408 | tf_op jit(solution)/shard_map/ppermute | solution.py:569
  384.5 51.4 %collective-permute-start.7 = (f32[320,2560]{1,0:T(8,128)}, f32[320,2560]{1,0:T(8,128)}, u32[]{:S(2)}, u32[]{:S(2)}) collective-permute-start(f32[320,2560]{1,0:T(8,128)} %get-tuple-element.43), channel_id=1, source_target_pairs={{0,1},{1,0},{2,3},{3,2},{4,5},{5,4},{6,7},{7,6},{8,9},{9,8},{10,11... | collective-permute-start | bytes 9830408 | tf_op jit(solution)/shard_map/ppermute | solution.py:569
  408.0 37.3 %collective-permute-start.6 = (f32[320,2560]{1,0:T(8,128)}, f32[320,2560]{1,0:T(8,128)S(1)}, u32[]{:S(2)}, u32[]{:S(2)}) collective-permute-start(f32[320,2560]{1,0:T(8,128)} %get-tuple-element.42), channel_id=1, source_target_pairs={{0,1},{1,0},{2,3},{3,2},{4,5},{5,4},{6,7},{7,6},{8,9},{9,8},{10,11... | collective-permute-start | bytes 9830408 | tf_op jit(solution)/shard_map/ppermute | solution.py:569
  408.6 80.0 %collective-permute-start.16 = (f32[640,1280]{1,0:T(8,128)}, f32[640,1280]{1,0:T(8,128)}, u32[]{:S(2)}, u32[]{:S(2)}) collective-permute-start(f32[640,1280]{1,0:T(8,128)} %get-tuple-element.44), channel_id=1, source_target_pairs={{0,1},{1,0},{2,3},{3,2},{4,5},{5,4},{6,7},{7,6},{8,9},{9,8},{10,11... | collective-permute-start | bytes 9830408 | tf_op jit(solution)/shard_map/ppermute | solution.py:569
  421.2 68.1 %collective-permute-start.20 = (f32[384,1280]{1,0:T(8,128)}, f32[384,1280]{1,0:T(8,128)}, u32[]{:S(2)}, u32[]{:S(2)}) collective-permute-start(f32[384,1280]{1,0:T(8,128)} %slice_add_fusion), channel_id=1, source_target_pairs={{0,2},{1,3},{2,0},{3,1},{4,6},{5,7},{6,4},{7,5},{8,10},{9,11},{10,... | collective-permute-start | bytes 5898248 | tf_op jit(solution)/shard_map/ppermute | solution.py:572
  440.3 44.5 %collective-permute-start.14 = (f32[320,640]{1,0:T(8,128)}, f32[320,640]{1,0:T(8,128)}, u32[]{:S(2)}, u32[]{:S(2)}) collective-permute-start(f32[320,640]{1,0:T(8,128)} %get-tuple-element.47), channel_id=1, source_target_pairs={{0,2},{1,3},{2,0},{3,1},{4,6},{5,7},{6,4},{7,5},{8,10},{9,11},{10,... | collective-permute-start | bytes 2457608 | tf_op jit(solution)/shard_map/ppermute | solution.py:572
  441.0 61.4 %collective-permute-start.12 = (f32[320,640]{1,0:T(8,128)S(1)}, f32[320,640]{1,0:T(8,128)}, u32[]{:S(2)}, u32[]{:S(2)}) collective-permute-start(f32[320,640]{1,0:T(8,128)S(1)} %get-tuple-element.48), channel_id=1, source_target_pairs={{0,2},{1,3},{2,0},{3,1},{4,6},{5,7},{6,4},{7,5},{8,10},{9,11},{10,... | collective-permute-start | bytes 2457608 | tf_op jit(solution)/shard_map/ppermute | solution.py:572
  445.2 14.4 %copy-start = (f32[320,2560]{1,0:T(8,128)}, f32[320,2560]{1,0:T(8,128)S(1)}, u32[]{:S(2)}) copy-start(f32[320,2560]{1,0:T(8,128)S(1)} %collective-permute-done.6.got_ref) | copy-start | bytes 9830404
  445.3 123.1 %collective-permute-start.18 = (f32[256,1280]{1,0:T(8,128)}, f32[256,1280]{1,0:T(8,128)}, u32[]{:S(2)}, u32[]{:S(2)}) collective-permute-start(f32[256,1280]{1,0:T(8,128)} %slice_add_fusion.1), channel_id=1, source_target_pairs={{0,2},{1,3},{2,0},{3,1},{4,6},{5,7},{6,4},{7,5},{8,10},{9,11},{10,... | collective-permute-start | bytes 3932168 | tf_op jit(solution)/shard_map/ppermute | solution.py:572
  484.8 63.1 %collective-permute-start.10 = (f32[320,640]{1,0:T(8,128)}, f32[320,640]{1,0:T(8,128)S(1)}, u32[]{:S(2)}, u32[]{:S(2)}) collective-permute-start(f32[320,640]{1,0:T(8,128)} %get-tuple-element.49), channel_id=1, source_target_pairs={{0,2},{1,3},{2,0},{3,1},{4,6},{5,7},{6,4},{7,5},{8,10},{9,11},{10,... | collective-permute-start | bytes 2457608 | tf_op jit(solution)/shard_map/ppermute | solution.py:572
  488.6 76.3 %collective-permute-start.8 = (f32[320,640]{1,0:T(8,128)}, f32[320,640]{1,0:T(8,128)S(1)}, u32[]{:S(2)}, u32[]{:S(2)}) collective-permute-start(f32[320,640]{1,0:T(8,128)} %get-tuple-element.46), channel_id=1, source_target_pairs={{0,2},{1,3},{2,0},{3,1},{4,6},{5,7},{6,4},{7,5},{8,10},{9,11},{10,... | collective-permute-start | bytes 2457608 | tf_op jit(solution)/shard_map/ppermute | solution.py:572
  489.3 83.2 %collective-permute-start.15 = (f32[320,640]{1,0:T(8,128)}, f32[320,640]{1,0:T(8,128)}, u32[]{:S(2)}, u32[]{:S(2)}) collective-permute-start(f32[320,640]{1,0:T(8,128)} %layer_sum.9), channel_id=1, source_target_pairs={{0,8},{8,0},{1,9},{9,1},{2,10},{10,2},{3,11},{11,3},{4,12},{12,4},... | collective-permute-start | bytes 2457608 | tf_op jit(solution)/shard_map/ppermute | solution.py:578
  502.4 128.8 %collective-permute-start.21 = (f32[384,1280]{1,0:T(8,128)}, f32[384,1280]{1,0:T(8,128)S(1)}, u32[]{:S(2)}, u32[]{:S(2)}) collective-permute-start(f32[384,1280]{1,0:T(8,128)} %layer_sum.11.refs_2_), channel_id=1, source_target_pairs={{0,8},{8,0},{1,9},{9,1},{2,10},{10,2},{3,11},{11,3},{4,12},{12,4},... | collective-permute-start | bytes 5898248 | tf_op jit(solution)/shard_map/ppermute | solution.py:578
  547.9 0.9 copy-start.9
  547.9 47.0 %collective-permute-start.13 = (f32[320,640]{1,0:T(8,128)}, f32[320,640]{1,0:T(8,128)}, u32[]{:S(2)}, u32[]{:S(2)}) collective-permute-start(f32[320,640]{1,0:T(8,128)} %layer_sum.8), channel_id=1, source_target_pairs={{0,8},{8,0},{1,9},{9,1},{2,10},{10,2},{3,11},{11,3},{4,12},{12,4},... | collective-permute-start | bytes 2457608 | tf_op jit(solution)/shard_map/ppermute | solution.py:578
  564.9 0.9 copy-start.8
  564.9 31.2 %collective-permute-start.11 = (f32[320,640]{1,0:T(8,128)}, f32[320,640]{1,0:T(8,128)}, u32[]{:S(2)}, u32[]{:S(2)}) collective-permute-start(f32[320,640]{1,0:T(8,128)} %layer_sum.7), channel_id=1, source_target_pairs={{0,8},{8,0},{1,9},{9,1},{2,10},{10,2},{3,11},{11,3},{4,12},{12,4},... | collective-permute-start | bytes 2457608 | tf_op jit(solution)/shard_map/ppermute | solution.py:578
  568.4 35.6 %collective-permute-start.9 = (f32[320,640]{1,0:T(8,128)}, f32[320,640]{1,0:T(8,128)}, u32[]{:S(2)}, u32[]{:S(2)}) collective-permute-start(f32[320,640]{1,0:T(8,128)} %layer_sum.6), channel_id=1, source_target_pairs={{0,8},{8,0},{1,9},{9,1},{2,10},{10,2},{3,11},{11,3},{4,12},{12,4},... | collective-permute-start | bytes 2457608 | tf_op jit(solution)/shard_map/ppermute | solution.py:578
  572.5 21.1 %copy-start.3 = (f32[320,640]{1,0:T(8,128)S(1)}, f32[320,640]{1,0:T(8,128)}, u32[]{:S(2)}) copy-start(f32[320,640]{1,0:T(8,128)} %layer_sum.9) | copy-start | bytes 2457604
  572.5 22.5 %copy-start.4 = (f32[320,640]{1,0:T(8,128)S(1)}, f32[320,640]{1,0:T(8,128)}, u32[]{:S(2)}) copy-start(f32[320,640]{1,0:T(8,128)} %layer_sum.8) | copy-start | bytes 2457604
  572.5 58.7 %collective-permute-start.19 = (f32[256,1280]{1,0:T(8,128)}, f32[256,1280]{1,0:T(8,128)}, u32[]{:S(2)}, u32[]{:S(2)}) collective-permute-start(f32[256,1280]{1,0:T(8,128)} %layer_sum.10.refs_0_), channel_id=1, source_target_pairs={{0,8},{8,0},{1,9},{9,1},{2,10},{10,2},{3,11},{11,3},{4,12},{12,4},... | collective-permute-start | bytes 3932168 | tf_op jit(solution)/shard_map/ppermute | solution.py:578
  593.5 2.6 copy-start.5
  593.6 10.4 %copy-start.6 = (f32[320,640]{1,0:T(8,128)S(1)}, f32[320,640]{1,0:T(8,128)}, u32[]{:S(2)}) copy-start(f32[320,640]{1,0:T(8,128)} %layer_sum.6) | copy-start | bytes 2457604
  631.2 1.3 copy-start.7

commit v2 on v1

--- a/solution.py
+++ b/solution.py
@@ -10,8 +10,7 @@
 VMEM_LIMIT = 60 * 1024 * 1024
 SQRT_2_OVER_PI = 0.7978845608028654
 CUBIC = 0.044715
-NCHUNK = 4
-NFIRST = 2
+NHALF = 2
 NPIECE1 = 4
 PER = 2
 NSLOT = 3
@@ -94,10 +93,9 @@
     late.append(start(tok_ref.at[pl.ds(0, first), :], tok_oth, to_col))
     late.append(start(w1_ref, place(0, x, col, col), to_core))
     late.append(start(w2_ref, place(1, x, col, col), to_core))
-    size = tok_oth.shape[0] // NFIRST
-    rest_of = tok_ref.shape[0] - NFIRST * size
+    size = tok_oth.shape[0]
     loads = [pltpu.make_async_copy(w1_ref, v1, load.at[0]), pltpu.make_async_copy(w2_ref, v2, load.at[1]),
-             pltpu.make_async_copy(tok_ref.at[pl.ds(NFIRST * size, rest_of), :], vt, load.at[2]),
+             pltpu.make_async_copy(tok_ref.at[pl.ds(size, size), :], vt, load.at[2]),
              pltpu.make_async_copy(grad_ref, vg, load.at[3])]
     for cp in loads:
         cp.start()
@@ -105,7 +103,7 @@
         cp.wait()
     keep = [pltpu.make_async_copy(v1, place(0, x, col, col), store.at[0]),
             pltpu.make_async_copy(v2, place(1, x, col, col), store.at[1])]
-    spans = [(vt, i) for i in range(NCHUNK - NFIRST)] + [(vg, i) for i in range(NCHUNK)]
+    spans = [(vt, 0)] + [(vg, i) for i in range(NHALF)]
     for j, (src, i) in enumerate(spans):
         keep.append(pltpu.make_async_copy(src.at[pl.ds(i * size, size), :], cut[j], store.at[2 + j]))
     for cp in keep:
@@ -153,7 +151,7 @@
 
 
 NCOPY = 25
-NCUT = 2 * NCHUNK - NFIRST
+NCUT = 1 + NHALF
 
 
 def gather_kernel(up, down, tok, grad, rows):
@@ -164,9 +162,9 @@
         out_specs=[pl.BlockSpec(memory_space=pl.ANY)] * (3 + NCUT),
         out_shape=[jax.ShapeDtypeStruct((4 * up.shape[0], 2 * up.shape[1]), BF16),
                    jax.ShapeDtypeStruct((4 * down.shape[0], 2 * down.shape[1]), BF16),
-                   jax.ShapeDtypeStruct((NFIRST * rows, tok.shape[1]), BF16)] + [piece] * NCUT,
+                   piece] + [piece] * NCUT,
         scratch_shapes=[pltpu.VMEM(up.shape, BF16), pltpu.VMEM(down.shape, BF16),
-                        pltpu.VMEM(((NCHUNK - NFIRST) * rows, tok.shape[1]), BF16), pltpu.VMEM(grad.shape, BF16),
+                        pltpu.VMEM((rows, tok.shape[1]), BF16), pltpu.VMEM(grad.shape, BF16),
                         pltpu.SemaphoreType.DMA((NCOPY,)), pltpu.SemaphoreType.DMA((NCOPY,)),
                         pltpu.SemaphoreType.DMA((4,)), pltpu.SemaphoreType.DMA((2 + NCUT,))],
         compiler_params=pltpu.CompilerParams(collective_id=0, has_side_effects=True, vmem_limit_bytes=VMEM_LIMIT),
@@ -178,7 +176,7 @@
 ANY = pl.BlockSpec(memory_space=pl.ANY)
 
 
-def make_up_body(first_row, nlater):
+def make_up_body(first_row, nlater, per):
     def up_body(xo_ref, *rest):
         xt_refs, w_ref = rest[:nlater], rest[nlater]
         a_hbm, d_hbm, x_ref, u0_ref, u1_ref, a_ref, d_ref, sem = rest[-8:]
@@ -186,13 +184,13 @@
         piece = u0_ref.shape[0]
         last = rows // piece - 1
         bn = w_ref.shape[1]
-        j, n = pl.program_id(0) * PER + pl.program_id(1), pl.num_programs(0) * PER
+        j, n = pl.program_id(0) * per + pl.program_id(1), pl.num_programs(0) * per
         row = pl.multiple_of(pl.program_id(1) * rows, rows)
 
         def copies(step, part):
             slot = lax.rem(step, NSLOT)
-            cols = pl.ds(pl.multiple_of(lax.div(step, PER) * bn, bn), bn)
-            base = pl.multiple_of(first_row + lax.rem(step, PER) * rows, rows)
+            cols = pl.ds(pl.multiple_of(lax.div(step, per) * bn, bn), bn)
+            base = pl.multiple_of(first_row + lax.rem(step, per) * rows, rows)
             first, size = ((0, last * piece), (last * piece, piece))[part]
             src, dst = pl.ds(first, size), pl.ds(base + first, size)
             return (pltpu.make_async_copy(a_ref.at[slot, src], a_hbm.at[dst, cols], sem.at[0, part, slot]),
@@ -260,10 +258,11 @@
     return up_body
 
 
-def up_kernel(x_own, x_oth, w1, rows, call, bufs, after, bn=512):
+def up_kernel(x_own, x_oth, w1, call, bufs, after, rows=512, bn=1024):
     tokens, hh = x_own.shape
     f = w1.shape[1]
-    in_specs = [pl.BlockSpec((PER * rows, hh), lambda j, i: (call, 0))]
+    total = sum(v.shape[0] for v in x_oth)
+    in_specs = [pl.BlockSpec((total, hh), lambda j, i: (call, 0))]
     in_specs += [pl.BlockSpec(v.shape, lambda j, i: (0, 0)) for v in x_oth]
     in_specs += [pl.BlockSpec((2 * hh, bn), lambda j, i: (0, j))]
     args = [x_own, *x_oth, w1]
@@ -273,16 +272,16 @@
         in_specs += [ANY] * 3
         args += [*bufs, after]
     return pl.pallas_call(
-        make_up_body(call * PER * rows, len(x_oth)),
-        grid=(f // bn, PER),
+        make_up_body(call * total, len(x_oth), total // rows),
+        grid=(f // bn, total // rows),
         in_specs=in_specs,
         out_specs=[ANY, ANY],
-        scratch_shapes=[pltpu.VMEM((PER * rows, 2 * hh), BF16), pltpu.VMEM((PIECE, bn), F32), pltpu.VMEM((PIECE, bn), F32),
+        scratch_shapes=[pltpu.VMEM((total, 2 * hh), BF16), pltpu.VMEM((PIECE, bn), F32), pltpu.VMEM((PIECE, bn), F32),
                         pltpu.VMEM((NSLOT, rows, bn), BF16), pltpu.VMEM((NSLOT, rows, bn), F32), pltpu.SemaphoreType.DMA((2, 2, NSLOT))],
         out_shape=[jax.ShapeDtypeStruct((tokens, f), BF16), jax.ShapeDtypeStruct((tokens, f), F32)],
         input_output_aliases=aliases,
         compiler_params=params(),
-        cost_estimate=cost(2 * PER * rows * 2 * hh * f, PER * rows * f * 6 + 2 * hh * f * 2, PER * rows * f),
+        cost_estimate=cost(2 * total * 2 * hh * f, total * f * 6 + 2 * hh * f * 2, total * f),
         name="up",
     )(*args)
 
@@ -582,25 +581,24 @@
         row = lax.axis_index("row")
         x, core = row // 2, row % 2
         tokens, hh = tok.shape
-        rows = tokens // NCHUNK
+        rows = tokens // NHALF
         fh = up.shape[1]
 
         w1, w2, tok_first, *cut = gather_kernel(up, down, tok, grad, rows)
-        nlater = NCHUNK - NFIRST
-        tok_later = [over_col(cut[i]) for i in range(nlater)]
-        grad_oth = [over_col(cut[nlater + i]) for i in range(NCHUNK)]
+        tok_later = over_col(cut[0])
+        grad_oth = [over_col(cut[1 + i]) for i in range(NHALF)]
 
         outs = {"y": None, "dx": None}
-        parts = {"y": ((0, 4), (4, 2), (6, 2)), "dx": ((0, 1), (1, 3), (4, 4))}
+        parts = {"y": ((0, 4), (4, 2), (6, 2)), "dx": ((0, 4), (4, 4))}
 
         def out_part(key, part, after=None):
             args = (y_body, "y", a, w2, (w2.shape[0], hh)) if key == "y" else (dx_body, "dx", du, w1, (hh, w1.shape[1]))
             outs[key] = out_kernel(*args, hh, *parts[key][part], outs[key], after)
             return outs[key]
 
-        a, d = up_kernel(tok, (tok_first,), w1, rows, 0, None, None)
+        a, d = up_kernel(tok, (tok_first,), w1, 0, None, None)
         dep = out_part("y", 0, w1)
-        a, d = up_kernel(tok, tok_later, w1, rows, 1, (a, d), dep)
+        a, d = up_kernel(tok, (tok_later,), w1, 1, (a, d), dep)
 
         away = dw2_kernel(jnp.stack([1 - x, core]), grad, a, fh, d)
         here = dw2_kernel(jnp.stack([x, core]), grad, a, fh, away[0])
@@ -615,11 +613,11 @@
         dw_down = fin2_kernel(pieces)
 
         du = None
-        for i in range(NCHUNK // PER):
-            du = du_kernel(grad, grad_oth[i * PER:(i + 1) * PER], w2, d, rows, i, du, here[0])
-
-        away = dw1_kernel(jnp.stack([(1 - x + col) % 2, col, core]), tok, (tok_first, *tok_later), du, fh, du)
-        here = dw1_kernel(jnp.stack([(x + col) % 2, col, core]), tok, (tok_first, *tok_later), du, fh, away[0])
+        for i in range(NHALF):
+            du = du_kernel(grad, (grad_oth[i],), w2, d, rows // PER, i, du, here[0])
+
+        away = dw1_kernel(jnp.stack([(1 - x + col) % 2, col, core]), tok, (tok_first, tok_later), du, fh, du)
+        here = dw1_kernel(jnp.stack([(x + col) % 2, col, core]), tok, (tok_first, tok_later), du, fh, away[0])
         got_away = over_core(away[1])
         got_here = over_core(here[1])
         cols = []
@@ -632,11 +630,10 @@
             cols.append(layer + over_depth(layer))
         dw_up = jnp.concatenate(cols, axis=1)
 
-        out_part("dx", 0, here[0])
-        out_part("y", 1, outs["dx"])
+        out_part("y", 1, here[0])
         out_part("y", 2)
-        out_part("dx", 1, outs["y"])
-        out_part("dx", 2)
+        out_part("dx", 0, outs["y"])
+        out_part("dx", 1)
         return outs["y"], outs["dx"], dw_up, dw_down
 
     return jax.shard_map(body, mesh=mesh, in_specs=(act_spec, weight_spec, weight_spec, act_spec),

time: 650 us -> 641 us (0.986); the launches traced: 639 us -> 640 us
  Pallas kernels: 491 us -> 501 us
  waiting for transfers between devices: 107 us -> 99.8 us
    pallas_call x2, Pallas kernels: 94.4 us -> 111 us  [up_kernel(): pl.pallas_call(make_up_body(call * total, len(x_oth), total // rows), gri...]
    pallas_call x6 -> x5, Pallas kernels: 94.4 us -> 88.4 us  [out_kernel(): pl.pallas_call(body, grid=(count,), in_specs=[pl.BlockSpec((bm, f), lambd...]
  transfers between devices with their start and end apart: 22 -> 19, of which waited for: 7 -> 6; matrix products, arithmetic and copies ran while one was open for 3% -> 3% of each run, Pallas kernels for 58% -> 59%
where the time goes in v2:
time: 641 us; the launch traced here: 640 us
  Pallas kernels  501 us (78%)
  waiting for transfers between devices  99.8 us (16%)
  other arithmetic  19.4 us (3%)
  starting transfers between devices  15.5 us (2%)
    pallas_call x1, Pallas kernels, gather_kernel(): pl.pallas_call(gather_body, in_specs=[pl.BlockSpec(memory_space=pl.ANY)]...  115 us
    pallas_call x2, Pallas kernels, up_kernel(): pl.pallas_call(make_up_body(call * total, len(x_oth), total // rows), gri...  111 us
    pallas_call x5, Pallas kernels, out_kernel(): pl.pallas_call(body, grid=(count,), in_specs=[pl.BlockSpec((bm, f), lambd...  88.4 us
    pallas_call x2, Pallas kernels, du_kernel(): pl.pallas_call(make_du_body(call * PER * rows, len(g_oth)), grid=(f // bn...  72.9 us
    ppermute x6, waiting for transfers between devices, over_x(): return lax.ppermute(v, 'row', x_pair)  69.4 us
    pallas_call x2, Pallas kernels, dw1_kernel(): pl.pallas_call(dw1_body, grid_spec=pltpu.PrefetchScalarGridSpec(num_scala...  46.8 us
    pallas_call x2, Pallas kernels, dw2_kernel(): pl.pallas_call(dw2_body, grid_spec=pltpu.PrefetchScalarGridSpec(num_scala...  43.2 us
    ppermute x6, waiting for transfers between devices, over_depth(): return lax.ppermute(v, 'depth', pair)  30.4 us
  transfers between devices with their start and end apart: 19, of which 6 were waited for; matrix products, arithmetic and copies ran while one was open for 3% of the time, Pallas kernels for 59%

profile of v2, /device:TPU:0, one launch (start us, length us, event | category | flops | bytes accessed | tf_op | source)
XLA Modules:
  0.0 640.1 jit_solution(11973153257855903905)
XLA Ops:
  0.6 115.4 %gather.1 = (bf16[1280,5120]{1,0:T(8,128)(2,1)}, bf16[5120,1280]{1,0:T(8,128)(2,1)}, bf16[2048,640]{1,0:T(8,128)(2,1)}, bf16[2048,640]{1,0:T(8,128)(2,1)}, bf16[...) custom-call(bf16[320,2560]{1,0:T(8,128)(2,1)} %w1_ref.1, bf16[1280,640]{1,0:T(8,128)(2,1)} %w2_ref.1, ...), custom_call_target="tpu_custom_call" | custom-call | bytes 300000000 | tf_op jit(solution)/shard_map/gather/pallas_call | solution.py:159
  116.0 1.4 collective-permute-start
  117.4 0.7 collective-permute-start.1
  118.1 1.4 collective-permute-start.2
  119.5 0.6 pad_add_fusion
  120.1 0.6 add_add_fusion
  120.7 55.4 %up.2 = (bf16[4096,5120]{1,0:T(8,128)(2,1)}, f32[4096,5120]{1,0:T(8,128)}) custom-call(bf16[4096,640]{1,0:T(8,128)(2,1)} %own_ref.3, bf16[2048,640]{1,0:T(8,128)(2,1)} %get-tuple-element.24.rest_0_, bf16[1280,5120]{1,0:T(8,128)(2,1)} %get-tuple-element.23.rest_1_.rest_0_.w_ref), custom_call_target="tpu_custom_call" | custom-call | flops 26843545600 | bytes 76021760 | tf_op jit(solution)/shard_map/up/pallas_call | solution.py:274
  176.1 22.1 %shard_map.75.rest_4_.rest_0_ = bf16[4096,640]{1,0:T(8,128)(2,1)} custom-call(bf16[4096,5120]{1,0:T(8,128)(2,1)} %get-tuple-element.25.a_ref.rest_2_, bf16[5120,1280]{1,0:T(8,128)(2,1)} %get-tuple-element.27.w_ref.rest_1_, bf16[1280,5120]{1,0:T(8,128)(2,1)} %get-tuple-element.23.rest_1_.rest_0_.w_ref), custom_call_target="tpu_custom_call" | custom-call | flops 13421772800 | bytes 27525120 | tf_op jit(solution)/shard_map/pallas_call | solution.py:372
  198.2 0.0 collective-permute-done.rest_0_.rest_1_
  198.2 1.5 copy-done.1
  199.7 55.2 %up.3 = (bf16[4096,5120]{1,0:T(8,128)(2,1)}, f32[4096,5120]{1,0:T(8,128)}) custom-call(bf16[4096,640]{1,0:T(8,128)(2,1)} %own_ref.3, bf16[2048,640]{1,0:T(8,128)(2,1)} %copy-done.1, bf16[1280,5120]{1,0:T(8,128)(2,1)} %get-tuple-element.23.rest_1_.rest_0_.w_ref, ...), custom_call_target="tpu_custom_call", output_to_operand_aliasing={{0}: (3, {}), {1}: (4, {})} | custom-call | flops 26843545600 | bytes 76021760 | tf_op jit(solution)/shard_map/up/pallas_call | solution.py:274
  255.0 21.5 %dw2.2 = (f32[640,1280]{1,0:T(8,128)}, f32[640,1280]{1,0:T(8,128)}) custom-call(s32[2]{0:T(128)} %get-tuple-element.47.s_ref, bf16[4096,640]{1,0:T(8,128)(2,1)} %go_ref.3, bf16[4096,5120]{1,0:T(8,128)(2,1)} %get-tuple-element.28.a_ref, f32[4096,5120]{1,0:T(8,128)} %get-tuple-element.30.dep_ref.rest_2_), custom_call_target="tpu_custom_call" | custom-call | flops 13421772800 | bytes 32768000 | tf_op jit(solution)/shard_map/dw2/pallas_call | solution.py:437
  276.5 0.0 collective-permute-start.14
  276.5 21.7 %dw2.3 = (f32[640,1280]{1,0:T(8,128)}, f32[640,1280]{1,0:T(8,128)}) custom-call(s32[2]{0:T(128)} %get-tuple-element.46.s_ref, bf16[4096,640]{1,0:T(8,128)(2,1)} %go_ref.3, bf16[4096,5120]{1,0:T(8,128)(2,1)} %get-tuple-element.28.a_ref, f32[640,1280]{1,0:T(8,128)} %get-tuple-element.32.dep_ref), custom_call_target="tpu_custom_call" | custom-call | flops 13421772800 | bytes 32768000 | tf_op jit(solution)/shard_map/dw2/pallas_call | solution.py:437
  298.2 0.0 collective-permute-done.2.rest_0_
  298.2 36.4 %du.2.rest_3_ = bf16[4096,5120]{1,0:T(8,128)(2,1)} custom-call(bf16[4096,640]{1,0:T(8,128)(2,1)} %go_ref.3, bf16[2048,640]{1,0:T(8,128)(2,1)} %collective-permute-done.2.rest_0_, bf16[5120,1280]{1,0:T(8,128)(2,1)} %get-tuple-element.27.w_ref.rest_1_, f32[4096,5120]{1,0:T(8,128)} %get-tuple-element.30.dep_ref.rest_2_, ...), custom_call_target="tpu_custom_call" | custom-call | flops 26843545600 | bytes 76021760 | tf_op jit(solution)/shard_map/du/pallas_call | solution.py:344
  334.7 36.5 %du.3.rest_2_.rest_3_.u_ref = bf16[4096,5120]{1,0:T(8,128)(2,1)} custom-call(bf16[4096,640]{1,0:T(8,128)(2,1)} %go_ref.3, bf16[2048,640]{1,0:T(8,128)(2,1)} %collective-permute-done.1.rest_0_, bf16[5120,1280]{1,0:T(8,128)(2,1)} %get-tuple-element.27.w_ref.rest_1_, f32[4096,5120]{1,0:T(8,128)} %get-tuple-element.30.dep_ref.rest_2_, ...), custom_call_target="tpu_custom_call", output_to_operand_aliasing={{}: (4, {})} | custom-call | flops 26843545600 | bytes 76021760 | tf_op jit(solution)/shard_map/du/pallas_call | solution.py:344
  371.2 23.3 %dw1.2 = (f32[320,2560]{1,0:T(8,128)}, f32[320,2560]{1,0:T(8,128)}) custom-call(s32[3]{0:T(128)} %get-tuple-element.45.s_ref, bf16[4096,640]{1,0:T(8,128)(2,1)} %own_ref.3, bf16[2048,640]{1,0:T(8,128)(2,1)} %get-tuple-element.24.rest_0_, bf16[2048,640]{1,0:T(8,128)(2,1)} %copy-done.1, bf16[4096,5120]{1,0:T(8,128)(2,1)} %du.3.rest_2_.rest_3_.u_ref, ...), custom_call_target="tpu_custom_call" | custom-call | flops 13421772800 | bytes 32768000 | tf_op jit(solution)/shard_map/dw1/pallas_call | solution.py:499
  394.5 0.7 collective-permute-start.4
  395.2 23.6 %dw1.3 = (f32[320,2560]{1,0:T(8,128)}, f32[320,2560]{1,0:T(8,128)}) custom-call(s32[3]{0:T(128)} %get-tuple-element.44.s_ref, bf16[4096,640]{1,0:T(8,128)(2,1)} %own_ref.3, bf16[2048,640]{1,0:T(8,128)(2,1)} %get-tuple-element.24.rest_0_, bf16[2048,640]{1,0:T(8,128)(2,1)} %copy-done.1, bf16[4096,5120]{1,0:T(8,128)(2,1)} %du.3.rest_2_.rest_3_.u_ref, ...), custom_call_target="tpu_custom_call" | custom-call | flops 13421772800 | bytes 32768000 | tf_op jit(solution)/shard_map/dw1/pallas_call | solution.py:499
  418.8 0.2 collective-permute-start.3
  419.0 0.3 collective-permute-start.13
  419.3 0.0 collective-permute-done.14
  419.3 3.6 slice_add_fusion
  423.0 0.6 collective-permute-start.17
  423.6 13.2 %shard_map.76.rest_0_ = bf16[4096,640]{1,0:T(8,128)(2,1)} custom-call(bf16[4096,5120]{1,0:T(8,128)(2,1)} %get-tuple-element.28.a_ref, bf16[5120,1280]{1,0:T(8,128)(2,1)} %get-tuple-element.27.w_ref.rest_1_, bf16[4096,640]{1,0:T(8,128)(2,1)} %shard_map.75.rest_4_.rest_0_, f32[320,2560]{1,0:T(8,128)} %get-tuple-element.35.rest_1_.here_ref), custom_call_target="tpu_custom_call", output_to_operand_aliasing={{}: (2, {})} | custom-call | flops 6710886400 | bytes 17039360 | tf_op jit(solution)/shard_map/pallas_call | solution.py:372
  436.9 4.4 slice_add_fusion.5
  441.3 1.4 collective-permute-start.11
  442.7 0.6 collective-permute-start.9
  443.3 2.9 slice_add_fusion.1
  446.2 0.0 collective-permute-done.3.got_ref
  446.2 1.4 collective-permute-start.15
  447.6 13.2 %shard_map.77.rest_0_ = bf16[4096,640]{1,0:T(8,128)(2,1)} custom-call(bf16[4096,5120]{1,0:T(8,128)(2,1)} %get-tuple-element.28.a_ref, bf16[5120,1280]{1,0:T(8,128)(2,1)} %get-tuple-element.27.w_ref.rest_1_, bf16[4096,640]{1,0:T(8,128)(2,1)} %shard_map.76.rest_0_), custom_call_target="tpu_custom_call", output_to_operand_aliasing={{}: (2, {})} | custom-call | flops 6710886400 | bytes 17039360 | tf_op jit(solution)/shard_map/pallas_call | solution.py:372
  460.9 25.7 %collective-permute-done.11.came_ref = f32[320,640]{1,0:T(8,128)} collective-permute-done((f32[320,640]{1,0:T(8,128)}, f32[320,640]{1,0:T(8,128)}, u32[]{:S(2)}, u32[]{:S(2)}) %collective-permute-start.11) | collective-permute-done | bytes 819232 | tf_op jit(solution)/shard_map/ppermute | solution.py:571
  486.5 0.6 collective-permute-start.7
  487.2 2.5 layer_sum.9
  489.7 1.4 collective-permute-start.5
  491.1 0.7 collective-permute-start.12
  491.7 4.6 layer_sum.11.refs_2_
  496.3 7.7 %collective-permute-done.9.came_ref = f32[320,640]{1,0:T(8,128)} collective-permute-done((f32[320,640]{1,0:T(8,128)S(1)}, f32[320,640]{1,0:T(8,128)}, u32[]{:S(2)}, u32[]{:S(2)}) %collective-permute-start.9) | collective-permute-done | bytes 819232 | tf_op jit(solution)/shard_map/ppermute | solution.py:571
  504.1 0.7 collective-permute-start.18
  504.8 19.9 %shard_map.78.rest_0_ = bf16[4096,640]{1,0:T(8,128)(2,1)} custom-call(bf16[4096,5120]{1,0:T(8,128)(2,1)} %du.3.rest_2_.rest_3_.u_ref, bf16[1280,5120]{1,0:T(8,128)(2,1)} %get-tuple-element.23.rest_1_.rest_0_.w_ref, bf16[4096,640]{1,0:T(8,128)(2,1)} %shard_map.77.rest_0_), custom_call_target="tpu_custom_call" | custom-call | flops 13421772800 | bytes 27525120 | tf_op jit(solution)/shard_map/pallas_call | solution.py:372
  524.7 2.4 layer_sum.8
  527.1 22.5 %collective-permute-done.7.came_ref = f32[320,640]{1,0:T(8,128)S(1)} collective-permute-done((f32[320,640]{1,0:T(8,128)}, f32[320,640]{1,0:T(8,128)S(1)}, u32[]{:S(2)}, u32[]{:S(2)}) %collective-permute-start.7) | collective-permute-done | bytes 819232 | tf_op jit(solution)/shard_map/ppermute | solution.py:571
  549.6 0.7 collective-permute-start.10
  550.3 0.2 copy-done.8
  550.5 2.5 layer_sum.7
  553.0 13.4 %collective-permute-done.5.came_ref = f32[320,640]{1,0:T(8,128)S(1)} collective-permute-done((f32[320,640]{1,0:T(8,128)}, f32[320,640]{1,0:T(8,128)S(1)}, u32[]{:S(2)}, u32[]{:S(2)}) %collective-permute-start.5) | collective-permute-done | bytes 819232 | tf_op jit(solution)/shard_map/ppermute | solution.py:571
  566.4 0.7 collective-permute-start.8
  567.0 0.3 copy-done.7
  567.3 2.5 layer_sum.6
  569.8 1.1 collective-permute-start.6
  570.9 3.0 layer_sum.10.refs_0_
  573.9 1.0 collective-permute-start.16
  574.9 19.9 %shard_map.79 = bf16[4096,640]{1,0:T(8,128)(2,1)} custom-call(bf16[4096,5120]{1,0:T(8,128)(2,1)} %du.3.rest_2_.rest_3_.u_ref, bf16[1280,5120]{1,0:T(8,128)(2,1)} %get-tuple-element.23.rest_1_.rest_0_.w_ref, bf16[4096,640]{1,0:T(8,128)(2,1)} %shard_map.78.rest_0_), custom_call_target="tpu_custom_call", output_to_operand_aliasing={{}: (2, {})} | custom-call | flops 13421772800 | bytes 27525120 | tf_op jit(solution)/shard_map/pallas_call | solution.py:372
  594.8 1.4 add.59
  596.2 1.2 add.57
  597.4 1.2 add.55
  598.6 6.7 %collective-permute-done.6 = f32[320,640]{1,0:T(8,128)} collective-permute-done((f32[320,640]{1,0:T(8,128)}, f32[320,640]{1,0:T(8,128)}, u32[]{:S(2)}, u32[]{:S(2)}) %collective-permute-start.6) | collective-permute-done | bytes 819232 | tf_op jit(solution)/shard_map/ppermute | solution.py:577
  605.4 1.2 add.53
  606.6 2.1 pad_maximum_fusion
  608.7 23.6 %collective-permute-done.16.refs_1_ = f32[256,1280]{1,0:T(8,128)} collective-permute-done((f32[256,1280]{1,0:T(8,128)}, f32[256,1280]{1,0:T(8,128)}, u32[]{:S(2)}, u32[]{:S(2)}) %collective-permute-start.16) | collective-permute-done | bytes 1310752 | tf_op jit(solution)/shard_map/ppermute | solution.py:577
  632.4 1.3 copy-done.6
  633.7 6.4 %fin2.1 = f32[1280,640]{1,0:T(8,128)} custom-call(f32[256,1280]{1,0:T(8,128)} %layer_sum.10.refs_0_, f32[256,1280]{1,0:T(8,128)} %collective-permute-done.16.refs_1_, f32[384,1280]{1,0:T(8,128)} %layer_sum.11.refs_2_, f32[384,1280]{1,0:T(8,128)} %copy-done.6), custom_call_target="tpu_custom_call" | custom-call | flops 819200 | bytes 9830400 | tf_op jit(solution)/shard_map/fin2/pallas_call | solution.py:547
  (23 shorter events, 0.0 us)
Async XLA Ops:
  116.0 82.2 %collective-permute-start = (bf16[2048,640]{1,0:T(8,128)(2,1)}, bf16[2048,640]{1,0:T(8,128)(2,1)S(1)}, u32[]{:S(2)}, u32[]{:S(2)}) collective-permute-start(bf16[2048,640]{1,0:T(8,128)(2,1)} %get-tuple-element.22), channel_id=1, source_target_pairs={{0,4},{4,0},{1,5},{5,1},{2,6},{6,2},{3,7},{7,3},{8,12},{12,8},{9,1... | collective-permute-start | bytes 7864328 | tf_op jit(solution)/shard_map/ppermute | solution.py:574
  117.4 217.2 %collective-permute-start.1 = (bf16[2048,640]{1,0:T(8,128)(2,1)}, bf16[2048,640]{1,0:T(8,128)(2,1)}, u32[]{:S(2)}, u32[]{:S(2)}) collective-permute-start(bf16[2048,640]{1,0:T(8,128)(2,1)} %get-tuple-element.29), channel_id=1, source_target_pairs={{0,4},{4,0},{1,5},{5,1},{2,6},{6,2},{3,7},{7,3},{8,12},{12,8},{9,1... | collective-permute-start | bytes 7864328 | tf_op jit(solution)/shard_map/ppermute | solution.py:574
  118.1 180.1 %collective-permute-start.2 = (bf16[2048,640]{1,0:T(8,128)(2,1)}, bf16[2048,640]{1,0:T(8,128)(2,1)}, u32[]{:S(2)}, u32[]{:S(2)}) collective-permute-start(bf16[2048,640]{1,0:T(8,128)(2,1)} %get-tuple-element.31), channel_id=1, source_target_pairs={{0,4},{4,0},{1,5},{5,1},{2,6},{6,2},{3,7},{7,3},{8,12},{12,8},{9,1... | collective-permute-start | bytes 7864328 | tf_op jit(solution)/shard_map/ppermute | solution.py:574
  198.2 1.5 copy-start.1
  276.5 142.8 %collective-permute-start.14 = (f32[640,1280]{1,0:T(8,128)}, f32[640,1280]{1,0:T(8,128)}, u32[]{:S(2)}, u32[]{:S(2)}) collective-permute-start(f32[640,1280]{1,0:T(8,128)} %get-tuple-element.39), channel_id=1, source_target_pairs={{0,1},{1,0},{2,3},{3,2},{4,5},{5,4},{6,7},{7,6},{8,9},{9,8},{10,11... | collective-permute-start | bytes 9830408 | tf_op jit(solution)/shard_map/ppermute | solution.py:568
  394.5 42.4 %collective-permute-start.4 = (f32[320,2560]{1,0:T(8,128)}, f32[320,2560]{1,0:T(8,128)}, u32[]{:S(2)}, u32[]{:S(2)}) collective-permute-start(f32[320,2560]{1,0:T(8,128)} %get-tuple-element.37), channel_id=1, source_target_pairs={{0,1},{1,0},{2,3},{3,2},{4,5},{5,4},{6,7},{7,6},{8,9},{9,8},{10,11... | collective-permute-start | bytes 9830408 | tf_op jit(solution)/shard_map/ppermute | solution.py:568
  418.8 27.4 %collective-permute-start.3 = (f32[320,2560]{1,0:T(8,128)}, f32[320,2560]{1,0:T(8,128)S(1)}, u32[]{:S(2)}, u32[]{:S(2)}) collective-permute-start(f32[320,2560]{1,0:T(8,128)} %get-tuple-element.36), channel_id=1, source_target_pairs={{0,1},{1,0},{2,3},{3,2},{4,5},{5,4},{6,7},{7,6},{8,9},{9,8},{10,11... | collective-permute-start | bytes 9830408 | tf_op jit(solution)/shard_map/ppermute | solution.py:568
  419.0 70.7 %collective-permute-start.13 = (f32[640,1280]{1,0:T(8,128)}, f32[640,1280]{1,0:T(8,128)}, u32[]{:S(2)}, u32[]{:S(2)}) collective-permute-start(f32[640,1280]{1,0:T(8,128)} %get-tuple-element.38), channel_id=1, source_target_pairs={{0,1},{1,0},{2,3},{3,2},{4,5},{5,4},{6,7},{7,6},{8,9},{9,8},{10,11... | collective-permute-start | bytes 9830408 | tf_op jit(solution)/shard_map/ppermute | solution.py:568
  423.0 68.1 %collective-permute-start.17 = (f32[384,1280]{1,0:T(8,128)}, f32[384,1280]{1,0:T(8,128)}, u32[]{:S(2)}, u32[]{:S(2)}) collective-permute-start(f32[384,1280]{1,0:T(8,128)} %slice_add_fusion), channel_id=1, source_target_pairs={{0,2},{1,3},{2,0},{3,1},{4,6},{5,7},{6,4},{7,5},{8,10},{9,11},{10,... | collective-permute-start | bytes 5898248 | tf_op jit(solution)/shard_map/ppermute | solution.py:571
  441.3 45.3 %collective-permute-start.11 = (f32[320,640]{1,0:T(8,128)}, f32[320,640]{1,0:T(8,128)}, u32[]{:S(2)}, u32[]{:S(2)}) collective-permute-start(f32[320,640]{1,0:T(8,128)} %get-tuple-element.41), channel_id=1, source_target_pairs={{0,2},{1,3},{2,0},{3,1},{4,6},{5,7},{6,4},{7,5},{8,10},{9,11},{10,... | collective-permute-start | bytes 2457608 | tf_op jit(solution)/shard_map/ppermute | solution.py:571
  442.7 61.4 %collective-permute-start.9 = (f32[320,640]{1,0:T(8,128)S(1)}, f32[320,640]{1,0:T(8,128)}, u32[]{:S(2)}, u32[]{:S(2)}) collective-permute-start(f32[320,640]{1,0:T(8,128)S(1)} %get-tuple-element.42), channel_id=1, source_target_pairs={{0,2},{1,3},{2,0},{3,1},{4,6},{5,7},{6,4},{7,5},{8,10},{9,11},{10,... | collective-permute-start | bytes 2457608 | tf_op jit(solution)/shard_map/ppermute | solution.py:571
  446.2 14.6 %copy-start = (f32[320,2560]{1,0:T(8,128)}, f32[320,2560]{1,0:T(8,128)S(1)}, u32[]{:S(2)}) copy-start(f32[320,2560]{1,0:T(8,128)S(1)} %collective-permute-done.3.got_ref) | copy-start | bytes 9830404
  446.2 123.5 %collective-permute-start.15 = (f32[256,1280]{1,0:T(8,128)}, f32[256,1280]{1,0:T(8,128)}, u32[]{:S(2)}, u32[]{:S(2)}) collective-permute-start(f32[256,1280]{1,0:T(8,128)} %slice_add_fusion.1), channel_id=1, source_target_pairs={{0,2},{1,3},{2,0},{3,1},{4,6},{5,7},{6,4},{7,5},{8,10},{9,11},{10,... | collective-permute-start | bytes 3932168 | tf_op jit(solution)/shard_map/ppermute | solution.py:571
  486.5 63.1 %collective-permute-start.7 = (f32[320,640]{1,0:T(8,128)}, f32[320,640]{1,0:T(8,128)S(1)}, u32[]{:S(2)}, u32[]{:S(2)}) collective-permute-start(f32[320,640]{1,0:T(8,128)} %get-tuple-element.43), channel_id=1, source_target_pairs={{0,2},{1,3},{2,0},{3,1},{4,6},{5,7},{6,4},{7,5},{8,10},{9,11},{10,... | collective-permute-start | bytes 2457608 | tf_op jit(solution)/shard_map/ppermute | solution.py:571
  489.7 76.7 %collective-permute-start.5 = (f32[320,640]{1,0:T(8,128)}, f32[320,640]{1,0:T(8,128)S(1)}, u32[]{:S(2)}, u32[]{:S(2)}) collective-permute-start(f32[320,640]{1,0:T(8,128)} %get-tuple-element.40), channel_id=1, source_target_pairs={{0,2},{1,3},{2,0},{3,1},{4,6},{5,7},{6,4},{7,5},{8,10},{9,11},{10,... | collective-permute-start | bytes 2457608 | tf_op jit(solution)/shard_map/ppermute | solution.py:571
  491.1 82.8 %collective-permute-start.12 = (f32[320,640]{1,0:T(8,128)}, f32[320,640]{1,0:T(8,128)}, u32[]{:S(2)}, u32[]{:S(2)}) collective-permute-start(f32[320,640]{1,0:T(8,128)} %layer_sum.9), channel_id=1, source_target_pairs={{0,8},{8,0},{1,9},{9,1},{2,10},{10,2},{3,11},{11,3},{4,12},{12,4},... | collective-permute-start | bytes 2457608 | tf_op jit(solution)/shard_map/ppermute | solution.py:577
  504.1 128.3 %collective-permute-start.18 = (f32[384,1280]{1,0:T(8,128)}, f32[384,1280]{1,0:T(8,128)S(1)}, u32[]{:S(2)}, u32[]{:S(2)}) collective-permute-start(f32[384,1280]{1,0:T(8,128)} %layer_sum.11.refs_2_), channel_id=1, source_target_pairs={{0,8},{8,0},{1,9},{9,1},{2,10},{10,2},{3,11},{11,3},{4,12},{12,4},... | collective-permute-start | bytes 5898248 | tf_op jit(solution)/shard_map/ppermute | solution.py:577
  549.6 0.9 copy-start.8
  549.6 46.5 %collective-permute-start.10 = (f32[320,640]{1,0:T(8,128)}, f32[320,640]{1,0:T(8,128)}, u32[]{:S(2)}, u32[]{:S(2)}) collective-permute-start(f32[320,640]{1,0:T(8,128)} %layer_sum.8), channel_id=1, source_target_pairs={{0,8},{8,0},{1,9},{9,1},{2,10},{10,2},{3,11},{11,3},{4,12},{12,4},... | collective-permute-start | bytes 2457608 | tf_op jit(solution)/shard_map/ppermute | solution.py:577
  566.4 0.9 copy-start.7
  566.4 31.0 %collective-permute-start.8 = (f32[320,640]{1,0:T(8,128)}, f32[320,640]{1,0:T(8,128)}, u32[]{:S(2)}, u32[]{:S(2)}) collective-permute-start(f32[320,640]{1,0:T(8,128)} %layer_sum.7), channel_id=1, source_target_pairs={{0,8},{8,0},{1,9},{9,1},{2,10},{10,2},{3,11},{11,3},{4,12},{12,4},... | collective-permute-start | bytes 2457608 | tf_op jit(solution)/shard_map/ppermute | solution.py:577
  569.8 35.6 %collective-permute-start.6 = (f32[320,640]{1,0:T(8,128)}, f32[320,640]{1,0:T(8,128)}, u32[]{:S(2)}, u32[]{:S(2)}) collective-permute-start(f32[320,640]{1,0:T(8,128)} %layer_sum.6), channel_id=1, source_target_pairs={{0,8},{8,0},{1,9},{9,1},{2,10},{10,2},{3,11},{11,3},{4,12},{12,4},... | collective-permute-start | bytes 2457608 | tf_op jit(solution)/shard_map/ppermute | solution.py:577
  573.9 20.9 %copy-start.2 = (f32[320,640]{1,0:T(8,128)S(1)}, f32[320,640]{1,0:T(8,128)}, u32[]{:S(2)}) copy-start(f32[320,640]{1,0:T(8,128)} %layer_sum.9) | copy-start | bytes 2457604
  573.9 22.2 %copy-start.3 = (f32[320,640]{1,0:T(8,128)S(1)}, f32[320,640]{1,0:T(8,128)}, u32[]{:S(2)}) copy-start(f32[320,640]{1,0:T(8,128)} %layer_sum.8) | copy-start | bytes 2457604
  573.9 58.5 %collective-permute-start.16 = (f32[256,1280]{1,0:T(8,128)}, f32[256,1280]{1,0:T(8,128)}, u32[]{:S(2)}, u32[]{:S(2)}) collective-permute-start(f32[256,1280]{1,0:T(8,128)} %layer_sum.10.refs_0_), channel_id=1, source_target_pairs={{0,8},{8,0},{1,9},{9,1},{2,10},{10,2},{3,11},{11,3},{4,12},{12,4},... | collective-permute-start | bytes 3932168 | tf_op jit(solution)/shard_map/ppermute | solution.py:577
  594.8 2.6 copy-start.4
  594.8 10.6 %copy-start.5 = (f32[320,640]{1,0:T(8,128)S(1)}, f32[320,640]{1,0:T(8,128)}, u32[]{:S(2)}) copy-start(f32[320,640]{1,0:T(8,128)} %layer_sum.6) | copy-start | bytes 2457604
  632.4 1.3 copy-start.6

commit v3 on v2

--- a/solution.py
+++ b/solution.py
@@ -11,7 +11,7 @@
 SQRT_2_OVER_PI = 0.7978845608028654
 CUBIC = 0.044715
 NHALF = 2
-NPIECE1 = 4
+WIDTHS = (1024, 1024, 512)
 PER = 2
 NSLOT = 3
 PIECE = 128
@@ -258,7 +258,7 @@
     return up_body
 
 
-def up_kernel(x_own, x_oth, w1, call, bufs, after, rows=512, bn=1024):
+def up_kernel(x_own, x_oth, w1, call, bufs, after, rows=1024, bn=512):
     tokens, hh = x_own.shape
     f = w1.shape[1]
     total = sum(v.shape[0] for v in x_oth)
@@ -621,13 +621,13 @@
         got_away = over_core(away[1])
         got_here = over_core(here[1])
         cols = []
-        w = fh // NPIECE1
-        for p in range(NPIECE1):
-            sl = slice(p * w, (p + 1) * w)
-            out = away[0][:, sl] + got_away[:, sl]
-            came = over_x(out)
-            layer = sum_kernel(here[0], got_here, came, lambda i, p=p: (i, p), 2)
+        at = 0
+        for w in WIDTHS:
+            sl = slice(at, at + w)
+            came = over_x(away[0][:, sl] + got_away[:, sl])
+            layer = sum_kernel(here[0], got_here, came, lambda i, q=at // w: (i, q), 2)
             cols.append(layer + over_depth(layer))
+            at += w
         dw_up = jnp.concatenate(cols, axis=1)
 
         out_part("y", 1, here[0])

time: 641 us -> 666 us (1.039)
  waiting for transfers between devices: 99.8 us -> 142 us
  Pallas kernels: 501 us -> 483 us
    ppermute x6 -> x5, waiting for transfers between devices: 30.4 us -> 67.3 us  [over_depth(): return lax.ppermute(v, 'depth', pair)]
    pallas_call x2, Pallas kernels: 111 us -> 94.4 us  [up_kernel(): pl.pallas_call(make_up_body(call * total, len(x_oth), total // rows), gri...]
    pallas_call x6 -> x5, Pallas kernels: 17.5 us -> 16 us  [sum_kernel(): pl.pallas_call(sum_body, grid=(steps,), in_specs=[pl.BlockSpec((bm, m), a...]
    ppermute x6 -> x5, waiting for transfers between devices: 69.4 us -> 68.4 us  [over_x(): return lax.ppermute(v, 'row', x_pair)]
  transfers between devices with their start and end apart: 19 -> 17, of which waited for: 6 -> 6; matrix products, arithmetic and copies ran while one was open for 3% -> 3% of each run, Pallas kernels for 59% -> 54%
where the time goes in v3:
time: 666 us; the launch traced here: 664 us
  Pallas kernels  483 us (73%)
  waiting for transfers between devices  142 us (21%)
  other arithmetic  21.6 us (3%)
  starting transfers between devices  14.2 us (2%)
    pallas_call x1, Pallas kernels, gather_kernel(): pl.pallas_call(gather_body, in_specs=[pl.BlockSpec(memory_space=pl.ANY)]...  115 us
    pallas_call x2, Pallas kernels, up_kernel(): pl.pallas_call(make_up_body(call * total, len(x_oth), total // rows), gri...  94.4 us
    pallas_call x5, Pallas kernels, out_kernel(): pl.pallas_call(body, grid=(count,), in_specs=[pl.BlockSpec((bm, f), lambd...  88.4 us
    pallas_call x2, Pallas kernels, du_kernel(): pl.pallas_call(make_du_body(call * PER * rows, len(g_oth)), grid=(f // bn...  72.9 us
    ppermute x5, waiting for transfers between devices, over_x(): return lax.ppermute(v, 'row', x_pair)  68.4 us
    ppermute x5, waiting for transfers between devices, over_depth(): return lax.ppermute(v, 'depth', pair)  67.3 us
    pallas_call x2, Pallas kernels, dw1_kernel(): pl.pallas_call(dw1_body, grid_spec=pltpu.PrefetchScalarGridSpec(num_scala...  46.5 us
    pallas_call x2, Pallas kernels, dw2_kernel(): pl.pallas_call(dw2_body, grid_spec=pltpu.PrefetchScalarGridSpec(num_scala...  43 us
  transfers between devices with their start and end apart: 17, of which 6 were waited for; matrix products, arithmetic and copies ran while one was open for 3% of the time, Pallas kernels for 54%

profile of v3, /device:TPU:0, one launch (start us, length us, event | category | flops | bytes accessed | tf_op | source)
XLA Modules:
  0.0 664.1 jit_solution(124727226914154290)
XLA Ops:
  0.6 115.4 %gather.1 = (bf16[1280,5120]{1,0:T(8,128)(2,1)}, bf16[5120,1280]{1,0:T(8,128)(2,1)}, bf16[2048,640]{1,0:T(8,128)(2,1)}, bf16[2048,640]{1,0:T(8,128)(2,1)}, bf16[...) custom-call(bf16[320,2560]{1,0:T(8,128)(2,1)} %w1_ref.1, bf16[1280,640]{1,0:T(8,128)(2,1)} %w2_ref.1, ...), custom_call_target="tpu_custom_call" | custom-call | bytes 300000000 | tf_op jit(solution)/shard_map/gather/pallas_call | solution.py:159
  116.0 1.4 collective-permute-start
  117.4 0.7 collective-permute-start.1
  118.1 1.4 collective-permute-start.2
  119.5 0.6 pad_add_fusion
  120.1 0.7 add_add_fusion
  120.8 47.2 %up.2 = (bf16[4096,5120]{1,0:T(8,128)(2,1)}, f32[4096,5120]{1,0:T(8,128)}) custom-call(bf16[4096,640]{1,0:T(8,128)(2,1)} %own_ref.3, bf16[2048,640]{1,0:T(8,128)(2,1)} %get-tuple-element.24.rest_0_, bf16[1280,5120]{1,0:T(8,128)(2,1)} %get-tuple-element.23.rest_1_.rest_0_.w_ref), custom_call_target="tpu_custom_call" | custom-call | flops 26843545600 | bytes 76021760 | tf_op jit(solution)/shard_map/up/pallas_call | solution.py:274
  168.0 22.1 %shard_map.75.rest_4_.rest_0_ = bf16[4096,640]{1,0:T(8,128)(2,1)} custom-call(bf16[4096,5120]{1,0:T(8,128)(2,1)} %get-tuple-element.25.a_ref.rest_2_, bf16[5120,1280]{1,0:T(8,128)(2,1)} %get-tuple-element.27.w_ref.rest_1_, bf16[1280,5120]{1,0:T(8,128)(2,1)} %get-tuple-element.23.rest_1_.rest_0_.w_ref), custom_call_target="tpu_custom_call" | custom-call | flops 13421772800 | bytes 27525120 | tf_op jit(solution)/shard_map/pallas_call | solution.py:372
  190.1 0.0 collective-permute-done.rest_0_.rest_1_
  190.1 1.5 copy-done.1
  191.6 47.2 %up.3 = (bf16[4096,5120]{1,0:T(8,128)(2,1)}, f32[4096,5120]{1,0:T(8,128)}) custom-call(bf16[4096,640]{1,0:T(8,128)(2,1)} %own_ref.3, bf16[2048,640]{1,0:T(8,128)(2,1)} %copy-done.1, bf16[1280,5120]{1,0:T(8,128)(2,1)} %get-tuple-element.23.rest_1_.rest_0_.w_ref, ...), custom_call_target="tpu_custom_call", output_to_operand_aliasing={{0}: (3, {}), {1}: (4, {})} | custom-call | flops 26843545600 | bytes 76021760 | tf_op jit(solution)/shard_map/up/pallas_call | solution.py:274
  238.8 21.5 %dw2.2 = (f32[640,1280]{1,0:T(8,128)}, f32[640,1280]{1,0:T(8,128)}) custom-call(s32[2]{0:T(128)} %get-tuple-element.45.s_ref, bf16[4096,640]{1,0:T(8,128)(2,1)} %go_ref.3, bf16[4096,5120]{1,0:T(8,128)(2,1)} %get-tuple-element.28.a_ref, f32[4096,5120]{1,0:T(8,128)} %get-tuple-element.30.dep_ref.rest_2_), custom_call_target="tpu_custom_call" | custom-call | flops 13421772800 | bytes 32768000 | tf_op jit(solution)/shard_map/dw2/pallas_call | solution.py:437
  260.3 0.0 collective-permute-start.12
  260.3 21.5 %dw2.3 = (f32[640,1280]{1,0:T(8,128)}, f32[640,1280]{1,0:T(8,128)}) custom-call(s32[2]{0:T(128)} %get-tuple-element.44.s_ref, bf16[4096,640]{1,0:T(8,128)(2,1)} %go_ref.3, bf16[4096,5120]{1,0:T(8,128)(2,1)} %get-tuple-element.28.a_ref, f32[640,1280]{1,0:T(8,128)} %get-tuple-element.32.dep_ref), custom_call_target="tpu_custom_call" | custom-call | flops 13421772800 | bytes 32768000 | tf_op jit(solution)/shard_map/dw2/pallas_call | solution.py:437
  281.8 6.1 collective-permute-done.2.rest_0_
  287.9 36.4 %du.2.rest_3_ = bf16[4096,5120]{1,0:T(8,128)(2,1)} custom-call(bf16[4096,640]{1,0:T(8,128)(2,1)} %go_ref.3, bf16[2048,640]{1,0:T(8,128)(2,1)} %collective-permute-done.2.rest_0_, bf16[5120,1280]{1,0:T(8,128)(2,1)} %get-tuple-element.27.w_ref.rest_1_, f32[4096,5120]{1,0:T(8,128)} %get-tuple-element.30.dep_ref.rest_2_, ...), custom_call_target="tpu_custom_call" | custom-call | flops 26843545600 | bytes 76021760 | tf_op jit(solution)/shard_map/du/pallas_call | solution.py:344
  324.3 0.0 collective-permute-done.1.rest_0_
  324.3 36.5 %du.3.rest_2_.rest_3_.u_ref = bf16[4096,5120]{1,0:T(8,128)(2,1)} custom-call(bf16[4096,640]{1,0:T(8,128)(2,1)} %go_ref.3, bf16[2048,640]{1,0:T(8,128)(2,1)} %collective-permute-done.1.rest_0_, bf16[5120,1280]{1,0:T(8,128)(2,1)} %get-tuple-element.27.w_ref.rest_1_, f32[4096,5120]{1,0:T(8,128)} %get-tuple-element.30.dep_ref.rest_2_, ...), custom_call_target="tpu_custom_call", output_to_operand_aliasing={{}: (4, {})} | custom-call | flops 26843545600 | bytes 76021760 | tf_op jit(solution)/shard_map/du/pallas_call | solution.py:344
  360.8 23.2 %dw1.2 = (f32[320,2560]{1,0:T(8,128)}, f32[320,2560]{1,0:T(8,128)}) custom-call(s32[3]{0:T(128)} %get-tuple-element.43.s_ref, bf16[4096,640]{1,0:T(8,128)(2,1)} %own_ref.3, bf16[2048,640]{1,0:T(8,128)(2,1)} %get-tuple-element.24.rest_0_, bf16[2048,640]{1,0:T(8,128)(2,1)} %copy-done.1, bf16[4096,5120]{1,0:T(8,128)(2,1)} %du.3.rest_2_.rest_3_.u_ref, ...), custom_call_target="tpu_custom_call" | custom-call | flops 13421772800 | bytes 32768000 | tf_op jit(solution)/shard_map/dw1/pallas_call | solution.py:499
  384.1 0.0 collective-permute-start.4
  384.1 23.2 %dw1.3 = (f32[320,2560]{1,0:T(8,128)}, f32[320,2560]{1,0:T(8,128)}) custom-call(s32[3]{0:T(128)} %get-tuple-element.42.s_ref, bf16[4096,640]{1,0:T(8,128)(2,1)} %own_ref.3, bf16[2048,640]{1,0:T(8,128)(2,1)} %get-tuple-element.24.rest_0_, bf16[2048,640]{1,0:T(8,128)(2,1)} %copy-done.1, bf16[4096,5120]{1,0:T(8,128)(2,1)} %du.3.rest_2_.rest_3_.u_ref, ...), custom_call_target="tpu_custom_call" | custom-call | flops 13421772800 | bytes 32768000 | tf_op jit(solution)/shard_map/dw1/pallas_call | solution.py:499
  407.4 0.7 collective-permute-start.3
  408.0 0.0 collective-permute-start.11
  408.1 0.0 collective-permute-done.12
  408.1 3.6 slice_add_fusion
  411.7 1.3 collective-permute-start.15
  413.1 13.2 %shard_map.76.rest_0_ = bf16[4096,640]{1,0:T(8,128)(2,1)} custom-call(bf16[4096,5120]{1,0:T(8,128)(2,1)} %get-tuple-element.28.a_ref, bf16[5120,1280]{1,0:T(8,128)(2,1)} %get-tuple-element.27.w_ref.rest_1_, bf16[4096,640]{1,0:T(8,128)(2,1)} %shard_map.75.rest_4_.rest_0_, f32[320,2560]{1,0:T(8,128)} %get-tuple-element.35.rest_1_.here_ref), custom_call_target="tpu_custom_call", output_to_operand_aliasing={{}: (2, {})} | custom-call | flops 6710886400 | bytes 17039360 | tf_op jit(solution)/shard_map/pallas_call | solution.py:372
  426.3 0.0 collective-permute-done.4
  426.3 4.8 slice_add_fusion.3
  431.1 0.7 collective-permute-start.7
  431.8 1.3 collective-permute-start.5
  433.1 13.2 %shard_map.77.rest_0_ = bf16[4096,640]{1,0:T(8,128)(2,1)} custom-call(bf16[4096,5120]{1,0:T(8,128)(2,1)} %get-tuple-element.28.a_ref, bf16[5120,1280]{1,0:T(8,128)(2,1)} %get-tuple-element.27.w_ref.rest_1_, bf16[4096,640]{1,0:T(8,128)(2,1)} %shard_map.76.rest_0_), custom_call_target="tpu_custom_call", output_to_operand_aliasing={{}: (2, {})} | custom-call | flops 6710886400 | bytes 17039360 | tf_op jit(solution)/shard_map/pallas_call | solution.py:372
  446.4 2.9 slice_add_fusion.1
  449.3 0.0 collective-permute-done.3.got_ref
  449.3 0.7 collective-permute-start.13
  450.0 2.7 slice_add_fusion.4
  452.7 33.1 %collective-permute-done.7.came_ref = f32[320,1024]{1,0:T(8,128)} collective-permute-done((f32[320,1024]{1,0:T(8,128)}, f32[320,1024]{1,0:T(8,128)}, u32[]{:S(2)}, u32[]{:S(2)}) %collective-permute-start.7) | collective-permute-done | bytes 1310752 | tf_op jit(solution)/shard_map/ppermute | solution.py:571
  485.8 1.3 collective-permute-start.9
  487.2 3.0 layer_sum.6
  490.2 23.7 %collective-permute-done.5.came_ref = f32[320,1024]{1,0:T(8,128)} collective-permute-done((f32[320,1024]{1,0:T(8,128)}, f32[320,1024]{1,0:T(8,128)}, u32[]{:S(2)}, u32[]{:S(2)}) %collective-permute-start.5) | collective-permute-done | bytes 1310752 | tf_op jit(solution)/shard_map/ppermute | solution.py:571
  513.9 0.5 collective-permute-start.8
  514.4 3.0 layer_sum.5
  517.5 0.0 collective-permute-done.11.got_ref
  517.5 1.5 collective-permute-start.6
  519.0 0.0 collective-permute-done.15.came_ref
  519.0 4.7 layer_sum.9.refs_2_
  523.6 0.5 collective-permute-start.16
  524.2 19.9 %shard_map.78.rest_0_ = bf16[4096,640]{1,0:T(8,128)(2,1)} custom-call(bf16[4096,5120]{1,0:T(8,128)(2,1)} %du.3.rest_2_.rest_3_.u_ref, bf16[1280,5120]{1,0:T(8,128)(2,1)} %get-tuple-element.23.rest_1_.rest_0_.w_ref, bf16[4096,640]{1,0:T(8,128)(2,1)} %shard_map.77.rest_0_), custom_call_target="tpu_custom_call" | custom-call | flops 13421772800 | bytes 27525120 | tf_op jit(solution)/shard_map/pallas_call | solution.py:372
  544.1 11.5 %collective-permute-done.9.came_ref = f32[320,512]{1,0:T(8,128)} collective-permute-done((f32[320,512]{1,0:T(8,128)}, f32[320,512]{1,0:T(8,128)}, u32[]{:S(2)}, u32[]{:S(2)}) %collective-permute-start.9) | collective-permute-done | bytes 655392 | tf_op jit(solution)/shard_map/ppermute | solution.py:571
  555.5 2.2 layer_sum.7
  557.8 0.5 collective-permute-start.10
  558.3 0.0 collective-permute-done.13.came_ref
  558.3 3.0 layer_sum.8.refs_0_
  561.3 1.5 collective-permute-start.14
  562.9 19.9 %shard_map.79 = bf16[4096,640]{1,0:T(8,128)(2,1)} custom-call(bf16[4096,5120]{1,0:T(8,128)(2,1)} %du.3.rest_2_.rest_3_.u_ref, bf16[1280,5120]{1,0:T(8,128)(2,1)} %get-tuple-element.23.rest_1_.rest_0_.w_ref, bf16[4096,640]{1,0:T(8,128)(2,1)} %shard_map.78.rest_0_), custom_call_target="tpu_custom_call", output_to_operand_aliasing={{}: (2, {})} | custom-call | flops 13421772800 | bytes 27525120 | tf_op jit(solution)/shard_map/pallas_call | solution.py:372
  582.8 47.4 %collective-permute-done.10 = f32[320,512]{1,0:T(8,128)} collective-permute-done((f32[320,512]{1,0:T(8,128)}, f32[320,512]{1,0:T(8,128)}, u32[]{:S(2)}, u32[]{:S(2)}) %collective-permute-start.10) | collective-permute-done | bytes 655392 | tf_op jit(solution)/shard_map/ppermute | solution.py:577
  630.1 1.2 add.51
  631.3 0.0 collective-permute-done.8
  631.4 1.5 add.49
  632.9 1.6 add.47
  634.5 2.0 pad_maximum_fusion
  636.5 19.9 %collective-permute-done.14.refs_1_ = f32[256,1280]{1,0:T(8,128)} collective-permute-done((f32[256,1280]{1,0:T(8,128)}, f32[256,1280]{1,0:T(8,128)}, u32[]{:S(2)}, u32[]{:S(2)}) %collective-permute-start.14) | collective-permute-done | bytes 1310752 | tf_op jit(solution)/shard_map/ppermute | solution.py:577
  656.4 1.3 copy-done.5
  657.7 6.4 fin2.1
  (12 shorter events, 0.0 us)
Async XLA Ops:
  116.0 74.1 %collective-permute-start = (bf16[2048,640]{1,0:T(8,128)(2,1)}, bf16[2048,640]{1,0:T(8,128)(2,1)S(1)}, u32[]{:S(2)}, u32[]{:S(2)}) collective-permute-start(bf16[2048,640]{1,0:T(8,128)(2,1)} %get-tuple-element.22), channel_id=1, source_target_pairs={{0,4},{4,0},{1,5},{5,1},{2,6},{6,2},{3,7},{7,3},{8,12},{12,8},{9,1... | collective-permute-start | bytes 7864328 | tf_op jit(solution)/shard_map/ppermute | solution.py:574
  117.4 206.9 %collective-permute-start.1 = (bf16[2048,640]{1,0:T(8,128)(2,1)}, bf16[2048,640]{1,0:T(8,128)(2,1)}, u32[]{:S(2)}, u32[]{:S(2)}) collective-permute-start(bf16[2048,640]{1,0:T(8,128)(2,1)} %get-tuple-element.29), channel_id=1, source_target_pairs={{0,4},{4,0},{1,5},{5,1},{2,6},{6,2},{3,7},{7,3},{8,12},{12,8},{9,1... | collective-permute-start | bytes 7864328 | tf_op jit(solution)/shard_map/ppermute | solution.py:574
  118.1 169.8 %collective-permute-start.2 = (bf16[2048,640]{1,0:T(8,128)(2,1)}, bf16[2048,640]{1,0:T(8,128)(2,1)}, u32[]{:S(2)}, u32[]{:S(2)}) collective-permute-start(bf16[2048,640]{1,0:T(8,128)(2,1)} %get-tuple-element.31), channel_id=1, source_target_pairs={{0,4},{4,0},{1,5},{5,1},{2,6},{6,2},{3,7},{7,3},{8,12},{12,8},{9,1... | collective-permute-start | bytes 7864328 | tf_op jit(solution)/shard_map/ppermute | solution.py:574
  190.1 1.5 copy-start.1
  260.3 147.8 %collective-permute-start.12 = (f32[640,1280]{1,0:T(8,128)}, f32[640,1280]{1,0:T(8,128)}, u32[]{:S(2)}, u32[]{:S(2)}) collective-permute-start(f32[640,1280]{1,0:T(8,128)} %get-tuple-element.39), channel_id=1, source_target_pairs={{0,1},{1,0},{2,3},{3,2},{4,5},{5,4},{6,7},{7,6},{8,9},{9,8},{10,11... | collective-permute-start | bytes 9830408 | tf_op jit(solution)/shard_map/ppermute | solution.py:568
  384.1 42.2 %collective-permute-start.4 = (f32[320,2560]{1,0:T(8,128)}, f32[320,2560]{1,0:T(8,128)}, u32[]{:S(2)}, u32[]{:S(2)}) collective-permute-start(f32[320,2560]{1,0:T(8,128)} %get-tuple-element.37), channel_id=1, source_target_pairs={{0,1},{1,0},{2,3},{3,2},{4,5},{5,4},{6,7},{7,6},{8,9},{9,8},{10,11... | collective-permute-start | bytes 9830408 | tf_op jit(solution)/shard_map/ppermute | solution.py:568
  407.4 41.9 %collective-permute-start.3 = (f32[320,2560]{1,0:T(8,128)}, f32[320,2560]{1,0:T(8,128)S(1)}, u32[]{:S(2)}, u32[]{:S(2)}) collective-permute-start(f32[320,2560]{1,0:T(8,128)} %get-tuple-element.36), channel_id=1, source_target_pairs={{0,1},{1,0},{2,3},{3,2},{4,5},{5,4},{6,7},{7,6},{8,9},{9,8},{10,11... | collective-permute-start | bytes 9830408 | tf_op jit(solution)/shard_map/ppermute | solution.py:568
  408.0 109.4 %collective-permute-start.11 = (f32[640,1280]{1,0:T(8,128)}, f32[640,1280]{1,0:T(8,128)}, u32[]{:S(2)}, u32[]{:S(2)}) collective-permute-start(f32[640,1280]{1,0:T(8,128)} %get-tuple-element.38), channel_id=1, source_target_pairs={{0,1},{1,0},{2,3},{3,2},{4,5},{5,4},{6,7},{7,6},{8,9},{9,8},{10,11... | collective-permute-start | bytes 9830408 | tf_op jit(solution)/shard_map/ppermute | solution.py:568
  411.7 107.2 %collective-permute-start.15 = (f32[384,1280]{1,0:T(8,128)}, f32[384,1280]{1,0:T(8,128)}, u32[]{:S(2)}, u32[]{:S(2)}) collective-permute-start(f32[384,1280]{1,0:T(8,128)} %slice_add_fusion), channel_id=1, source_target_pairs={{0,2},{1,3},{2,0},{3,1},{4,6},{5,7},{6,4},{7,5},{8,10},{9,11},{10,... | collective-permute-start | bytes 5898248 | tf_op jit(solution)/shard_map/ppermute | solution.py:571
  431.1 54.7 %collective-permute-start.7 = (f32[320,1024]{1,0:T(8,128)}, f32[320,1024]{1,0:T(8,128)}, u32[]{:S(2)}, u32[]{:S(2)}) collective-permute-start(f32[320,1024]{1,0:T(8,128)} %get-tuple-element.41), channel_id=1, source_target_pairs={{0,2},{1,3},{2,0},{3,1},{4,6},{5,7},{6,4},{7,5},{8,10},{9,11},{10,... | collective-permute-start | bytes 3932168 | tf_op jit(solution)/shard_map/ppermute | solution.py:571
  431.8 82.1 %collective-permute-start.5 = (f32[320,1024]{1,0:T(8,128)}, f32[320,1024]{1,0:T(8,128)}, u32[]{:S(2)}, u32[]{:S(2)}) collective-permute-start(f32[320,1024]{1,0:T(8,128)} %get-tuple-element.40), channel_id=1, source_target_pairs={{0,2},{1,3},{2,0},{3,1},{4,6},{5,7},{6,4},{7,5},{8,10},{9,11},{10,... | collective-permute-start | bytes 3932168 | tf_op jit(solution)/shard_map/ppermute | solution.py:571
  449.3 37.9 %copy-start = (f32[320,2560]{1,0:T(8,128)}, f32[320,2560]{1,0:T(8,128)S(1)}, u32[]{:S(2)}) copy-start(f32[320,2560]{1,0:T(8,128)S(1)} %collective-permute-done.3.got_ref) | copy-start | bytes 9830404
  449.3 109.0 %collective-permute-start.13 = (f32[256,1280]{1,0:T(8,128)}, f32[256,1280]{1,0:T(8,128)}, u32[]{:S(2)}, u32[]{:S(2)}) collective-permute-start(f32[256,1280]{1,0:T(8,128)} %slice_add_fusion.1), channel_id=1, source_target_pairs={{0,2},{1,3},{2,0},{3,1},{4,6},{5,7},{6,4},{7,5},{8,10},{9,11},{10,... | collective-permute-start | bytes 3932168 | tf_op jit(solution)/shard_map/ppermute | solution.py:571
  485.8 69.7 %collective-permute-start.9 = (f32[320,512]{1,0:T(8,128)}, f32[320,512]{1,0:T(8,128)}, u32[]{:S(2)}, u32[]{:S(2)}) collective-permute-start(f32[320,512]{1,0:T(8,128)} %slice_add_fusion.4), channel_id=1, source_target_pairs={{0,2},{1,3},{2,0},{3,1},{4,6},{5,7},{6,4},{7,5},{8,10},{9,11},{10,... | collective-permute-start | bytes 1966088 | tf_op jit(solution)/shard_map/ppermute | solution.py:571
  513.9 117.4 %collective-permute-start.8 = (f32[320,1024]{1,0:T(8,128)}, f32[320,1024]{1,0:T(8,128)}, u32[]{:S(2)}, u32[]{:S(2)}) collective-permute-start(f32[320,1024]{1,0:T(8,128)} %layer_sum.6), channel_id=1, source_target_pairs={{0,8},{8,0},{1,9},{9,1},{2,10},{10,2},{3,11},{11,3},{4,12},{12,4},... | collective-permute-start | bytes 3932168 | tf_op jit(solution)/shard_map/ppermute | solution.py:577
  517.5 115.4 %collective-permute-start.6 = (f32[320,1024]{1,0:T(8,128)}, f32[320,1024]{1,0:T(8,128)}, u32[]{:S(2)}, u32[]{:S(2)}) collective-permute-start(f32[320,1024]{1,0:T(8,128)} %layer_sum.5), channel_id=1, source_target_pairs={{0,8},{8,0},{1,9},{9,1},{2,10},{10,2},{3,11},{11,3},{4,12},{12,4},... | collective-permute-start | bytes 3932168 | tf_op jit(solution)/shard_map/ppermute | solution.py:577
  523.6 132.7 %collective-permute-start.16 = (f32[384,1280]{1,0:T(8,128)}, f32[384,1280]{1,0:T(8,128)S(1)}, u32[]{:S(2)}, u32[]{:S(2)}) collective-permute-start(f32[384,1280]{1,0:T(8,128)} %layer_sum.9.refs_2_), channel_id=1, source_target_pairs={{0,8},{8,0},{1,9},{9,1},{2,10},{10,2},{3,11},{11,3},{4,12},{12,4},... | collective-permute-start | bytes 5898248 | tf_op jit(solution)/shard_map/ppermute | solution.py:577
  557.8 72.4 %collective-permute-start.10 = (f32[320,512]{1,0:T(8,128)}, f32[320,512]{1,0:T(8,128)}, u32[]{:S(2)}, u32[]{:S(2)}) collective-permute-start(f32[320,512]{1,0:T(8,128)} %layer_sum.7), channel_id=1, source_target_pairs={{0,8},{8,0},{1,9},{9,1},{2,10},{10,2},{3,11},{11,3},{4,12},{12,4},... | collective-permute-start | bytes 1966088 | tf_op jit(solution)/shard_map/ppermute | solution.py:577
  561.3 68.8 %copy-start.4 = (f32[320,512]{1,0:T(8,128)S(1)}, f32[320,512]{1,0:T(8,128)}, u32[]{:S(2)}) copy-start(f32[320,512]{1,0:T(8,128)} %layer_sum.7) | copy-start | bytes 1966084
  561.3 70.0 %copy-start.2 = (f32[320,1024]{1,0:T(8,128)S(1)}, f32[320,1024]{1,0:T(8,128)}, u32[]{:S(2)}) copy-start(f32[320,1024]{1,0:T(8,128)} %layer_sum.6) | copy-start | bytes 3932164
  561.3 95.0 %collective-permute-start.14 = (f32[256,1280]{1,0:T(8,128)}, f32[256,1280]{1,0:T(8,128)}, u32[]{:S(2)}, u32[]{:S(2)}) collective-permute-start(f32[256,1280]{1,0:T(8,128)} %layer_sum.8.refs_0_), channel_id=1, source_target_pairs={{0,8},{8,0},{1,9},{9,1},{2,10},{10,2},{3,11},{11,3},{4,12},{12,4},... | collective-permute-start | bytes 3932168 | tf_op jit(solution)/shard_map/ppermute | solution.py:577
  582.8 50.2 %copy-start.3 = (f32[320,1024]{1,0:T(8,128)S(1)}, f32[320,1024]{1,0:T(8,128)}, u32[]{:S(2)}) copy-start(f32[320,1024]{1,0:T(8,128)} %layer_sum.5) | copy-start | bytes 3932164
  656.4 1.3 copy-start.5
